TPU v7x, 8 devices: a whole 2x2x1 slice. The times are simulated.
8 devices in a mesh: rep: 1 (over z), dp: 8 (over x, y, core).
Axes of the slice: x: 2, y: 2, z: 1, core: 2. Of those that a mesh axis runs over, the one named last changes fastest.
Arguments:
- g_w_gate: bfloat16 [8, 2, 1280, 4480], P(('rep', 'dp'))
- g_w_up: bfloat16 [8, 2, 1280, 4480], P(('rep', 'dp'))
- g_w_down: bfloat16 [8, 2, 4480, 1280], P(('rep', 'dp'))
- w_gate: bfloat16 [2, 1280, 4480], replicated
- w_up: bfloat16 [2, 1280, 4480], replicated
- w_down: bfloat16 [2, 4480, 1280], replicated
- m_w_gate: float32 [2, 1280, 4480], P(None, 'dp')
- m_w_up: float32 [2, 1280, 4480], P(None, 'dp')
- m_w_down: float32 [2, 4480, 1280], P(None, 'dp')
- v_w_gate: float32 [2, 1280, 4480], P(None, 'dp')
- v_w_up: float32 [2, 1280, 4480], P(None, 'dp')
- v_w_down: float32 [2, 4480, 1280], P(None, 'dp')
Outputs:
- output 1: bfloat16 [2, 1280, 4480], P('rep')
- output 2: bfloat16 [2, 1280, 4480], P('rep')
- output 3: bfloat16 [2, 4480, 1280], P('rep')
- output 4: float32 [2, 1280, 4480], P('rep', 'dp')
- output 5: float32 [2, 1280, 4480], P('rep', 'dp')
- output 6: float32 [2, 4480, 1280], P('rep', 'dp')
- output 7: float32 [2, 1280, 4480], P('rep', 'dp')
- output 8: float32 [2, 1280, 4480], P('rep', 'dp')
- output 9: float32 [2, 4480, 1280], P('rep', 'dp')
All inputs are finite; a program needn't handle non-finite values.
Results may differ from a plain program's by a relative error of at most 0.022.
Values are sent between devices in bfloat16 or wider.
A program may use at most 2 GiB of HBM per device.

v0:
```python
import jax
import jax.numpy as jnp
from jax import lax
from jax.sharding import PartitionSpec as P


def adamw(w, m, v, g):
    m = 0.9 * m + 0.1 * g
    v = 0.95 * v + 0.05 * g * g
    step = m * lax.rsqrt(v + 1e-8) + 0.1 * w
    return (w - 0.02 * step).astype(jnp.bfloat16), m, v


def solution(mesh):
    def step(*arrays):
        terms, weights, m, v = (arrays[i : i + 3] for i in (0, 3, 6, 9))
        gradients = [lax.psum_scatter(t[0], "dp", scatter_dimension=1, tiled=True).astype(jnp.float32) for t in terms]
        me = lax.axis_index("dp")
        own = [lax.dynamic_slice_in_dim(w, me * one.shape[1], one.shape[1], 1).astype(jnp.float32) for w, one in zip(weights, m, strict=True)]
        new = [adamw(w, m, v, g) for w, m, v, g in zip(own, m, v, gradients, strict=True)]
        whole = [lax.all_gather(one[0], "dp", axis=1, tiled=True) for one in new]
        return (*whole, *(one[1] for one in new), *(one[2] for one in new))

    all_of, cut = P(None, None, None), P(None, "dp", None)
    return jax.shard_map(
        step,
        mesh=mesh,
        in_specs=(P(("rep", "dp"), None, None, None),) * 3 + (all_of,) * 3 + (cut,) * 6,
        out_specs=(P("rep", None, None),) * 3 + (P("rep", "dp", None),) * 6,
        check_vma=False,
    )
```

profile of v0, /device:TPU:0, one launch (start us, length us, event | category | flops | bytes accessed | tf_op | source)
XLA Modules:
  0.0 820.2 jit_solution(3998082175111209416)
XLA Ops:
  7.2 0.0 reduce-scatter.8.cloned.1.call-start
  7.2 0.7 reduce-scatter.8.cloned.1.call-update
  7.9 0.0 reduce-scatter.6.cloned.1.call-start
  8.0 0.7 reduce-scatter.6.cloned.1.call-update
  8.7 0.0 reduce-scatter.4.cloned.1.call-start
  8.7 0.7 reduce-scatter.4.cloned.1.call-update
  9.4 0.0 all-gather.8.cloned.1.call-start
  9.4 141.1 %reduce-scatter.8.cloned.1.call-done = bf16[2,560,1280]{2,1,0:T(8,128)(2,1)} async-done(((bf16[2,4480,1280]{2,1,0:T(8,128)(2,1)}), bf16[2,560,1280]{2,1,0:T(8,128)(2,1)}) %reduce-scatter.8.cloned.1.call-update) | async-done | bytes 2867216 | tf_op jit(solution)/shard_map/reduce_scatter | solution.py:17
  150.5 11.9 %fusion.10 = (bf16[2,560,1280]{2,1,0:T(8,128)(2,1)}, f32[2,560,1280]{2,1,0:T(8,128)}, f32[2,560,1280]{2,1,0:T(8,128)}) fusion(bf16[2,4480,1280]{2,1,0:T(8,128)(2,1)} %param.17, s32[]{:T(128)S(6)} %select_n.8, bf16[2,560,1280]{2,1,0:T(8,128)(2,1)} %reduce-scatter.8.cloned.1.call-done, f32[2,560,1280]{2,1,0:T(8,128)} %param.23, f32[2,560,1280]{2,1,0:T(8,128)} %param.20), kind=kLoop, calls=%fused_computation.22 | loop fusion | flops 22937600 | bytes 31539204 | tf_op jit(solution)/shard_map/convert_element_type | solution.py:11
  162.4 0.0 all-gather.8.cloned.1.call-update
  162.4 0.0 all-gather.6.cloned.1.call-start
  162.5 127.8 %reduce-scatter.6.cloned.1.call-done = bf16[2,160,4480]{2,1,0:T(8,128)(2,1)} async-done(((bf16[2,1280,4480]{2,1,0:T(8,128)(2,1)}), bf16[2,160,4480]{2,1,0:T(8,128)(2,1)}) %reduce-scatter.6.cloned.1.call-update) | async-done | bytes 2867216 | tf_op jit(solution)/shard_map/reduce_scatter | solution.py:17
  290.3 11.9 %fusion.6 = (bf16[2,160,4480]{2,1,0:T(8,128)(2,1)}, f32[2,160,4480]{2,1,0:T(8,128)}, f32[2,160,4480]{2,1,0:T(8,128)}) fusion(bf16[2,1280,4480]{2,1,0:T(8,128)(2,1)} %param.16, s32[]{:T(128)S(6)} %select_n.7, bf16[2,160,4480]{2,1,0:T(8,128)(2,1)} %reduce-scatter.6.cloned.1.call-done, f32[2,160,4480]{2,1,0:T(8,128)} %param.22, f32[2,160,4480]{2,1,0:T(8,128)} %param.19), kind=kLoop, calls=%fused_computation.18 | loop fusion | flops 22937600 | bytes 31539204 | tf_op jit(solution)/shard_map/convert_element_type | solution.py:11
  302.1 0.0 all-gather.6.cloned.1.call-update
  302.2 0.0 all-gather.4.cloned.1.call-start
  302.2 127.8 %reduce-scatter.4.cloned.1.call-done = bf16[2,160,4480]{2,1,0:T(8,128)(2,1)} async-done(((bf16[2,1280,4480]{2,1,0:T(8,128)(2,1)}), bf16[2,160,4480]{2,1,0:T(8,128)(2,1)}) %reduce-scatter.4.cloned.1.call-update) | async-done | bytes 2867216 | tf_op jit(solution)/shard_map/reduce_scatter | solution.py:17
  430.0 11.9 %fusion.2 = (bf16[2,160,4480]{2,1,0:T(8,128)(2,1)}, f32[2,160,4480]{2,1,0:T(8,128)}, f32[2,160,4480]{2,1,0:T(8,128)}) fusion(bf16[2,1280,4480]{2,1,0:T(8,128)(2,1)} %param.15, s32[]{:T(128)S(6)} %select_n.7, bf16[2,160,4480]{2,1,0:T(8,128)(2,1)} %reduce-scatter.4.cloned.1.call-done, f32[2,160,4480]{2,1,0:T(8,128)} %param.21, f32[2,160,4480]{2,1,0:T(8,128)} %param.18), kind=kLoop, calls=%fused_computation.14 | loop fusion | flops 22937600 | bytes 31539204 | tf_op jit(solution)/shard_map/convert_element_type | solution.py:11
  441.9 0.0 all-gather.4.cloned.1.call-update
  441.9 100.6 %all-gather.8.cloned.1.call-done = bf16[2,4480,1280]{2,1,0:T(8,128)(2,1)} async-done(((bf16[2,560,1280]{2,1,0:T(8,128)(2,1)}), bf16[2,4480,1280]{2,1,0:T(8,128)(2,1)}) %all-gather.8.cloned.1.call-update) | async-done | bytes 22937616 | tf_op jit(solution)/shard_map/all_gather | solution.py:21
  542.5 112.5 %all-gather.6.cloned.1.call-done = bf16[2,1280,4480]{2,1,0:T(8,128)(2,1)} async-done(((bf16[2,160,4480]{2,1,0:T(8,128)(2,1)}), bf16[2,1280,4480]{2,1,0:T(8,128)(2,1)}) %all-gather.6.cloned.1.call-update) | async-done | bytes 22937616 | tf_op jit(solution)/shard_map/all_gather | solution.py:21
  655.0 112.5 %all-gather.4.cloned.1.call-done = bf16[2,1280,4480]{2,1,0:T(8,128)(2,1)} async-done(((bf16[2,160,4480]{2,1,0:T(8,128)(2,1)}), bf16[2,1280,4480]{2,1,0:T(8,128)(2,1)}) %all-gather.4.cloned.1.call-update) | async-done | bytes 22937616 | tf_op jit(solution)/shard_map/all_gather | solution.py:21
  767.5 19.0 %copy.24 = bf16[2,1280,4480]{2,1,0:T(8,128)(2,1)} copy(bf16[2,1280,4480]{2,1,0:T(8,128)(2,1)} %all-gather.4.cloned.1.call-done) | data formatting | bytes 45875200
  786.5 18.7 %copy.25 = bf16[2,1280,4480]{2,1,0:T(8,128)(2,1)} copy(bf16[2,1280,4480]{2,1,0:T(8,128)(2,1)} %all-gather.6.cloned.1.call-done) | data formatting | bytes 45875200
  805.2 8.2 copy.26
  (13 shorter events, 0.0 us)
Async XLA Ops:
  7.2 143.4 %reduce-scatter.8.cloned.1.call-start = ((), (), s32[]{:S(2)}) async-start(), calls=%async_computation.7 | async-start | bytes 25804800 | tf_op jit(solution)/shard_map/reduce_scatter | solution.py:17
  7.9 282.4 %reduce-scatter.6.cloned.1.call-start = ((), (), s32[]{:S(2)}) async-start(), calls=%async_computation.5 | async-start | bytes 25804800 | tf_op jit(solution)/shard_map/reduce_scatter | solution.py:17
  8.7 421.3 %reduce-scatter.4.cloned.1.call-start = ((), (), s32[]{:S(2)}) async-start(), calls=%async_computation.3 | async-start | bytes 25804800 | tf_op jit(solution)/shard_map/reduce_scatter | solution.py:17
  9.4 533.1 %all-gather.8.cloned.1.call-start = ((), (), s32[]{:S(2)}) async-start(), calls=%async_computation.8 | async-start | bytes 25804800 | tf_op jit(solution)/shard_map/all_gather | solution.py:21
  162.4 492.5 %all-gather.6.cloned.1.call-start = ((), (), s32[]{:S(2)}) async-start(), calls=%async_computation.6 | async-start | bytes 25804800 | tf_op jit(solution)/shard_map/all_gather | solution.py:21
  302.2 465.3 %all-gather.4.cloned.1.call-start = ((), (), s32[]{:S(2)}) async-start(), calls=%async_computation.4 | async-start | bytes 25804800 | tf_op jit(solution)/shard_map/all_gather | solution.py:21
  767.5 37.7 %slice-start = ((s8[22937600]{0:T(1024)(128)(4,1)}), s8[4194304]{0:T(1024)(128)(4,1)S(1)}, s32[]{:S(2)}) async-start(s8[22937600]{0:T(1024)(128)(4,1)} %bitcast.6), calls=%async_computation.9 | async-start | bytes 8388608
  767.5 37.7 %slice-start.1 = ((s8[22937600]{0:T(1024)(128)(4,1)}), s8[4194304]{0:T(1024)(128)(4,1)S(1)}, s32[]{:S(2)}) async-start(s8[22937600]{0:T(1024)(128)(4,1)} %bitcast.6), calls=%async_computation.10 | async-start | bytes 8388608
  767.5 37.7 %slice-start.2 = ((s8[22937600]{0:T(1024)(128)(4,1)}), s8[4194304]{0:T(1024)(128)(4,1)S(1)}, s32[]{:S(2)}) async-start(s8[22937600]{0:T(1024)(128)(4,1)} %bitcast.6), calls=%async_computation.11 | async-start | bytes 8388608
  786.5 18.7 %slice-start.3 = ((s8[22937600]{0:T(1024)(128)(4,1)}), s8[4194304]{0:T(1024)(128)(4,1)S(1)}, s32[]{:S(2)}) async-start(s8[22937600]{0:T(1024)(128)(4,1)} %bitcast.6), calls=%async_computation.12 | async-start | bytes 8388608
  786.5 18.7 %slice-start.4 = ((s8[22937600]{0:T(1024)(128)(4,1)}), s8[4194304]{0:T(1024)(128)(4,1)S(1)}, s32[]{:S(2)}) async-start(s8[22937600]{0:T(1024)(128)(4,1)} %bitcast.6), calls=%async_computation.13 | async-start | bytes 8388608
  786.5 18.7 %slice-start.5 = ((s8[22937600]{0:T(1024)(128)(4,1)}), s8[1966080]{0:T(1024)(128)(4,1)S(1)}, s32[]{:S(2)}) async-start(s8[22937600]{0:T(1024)(128)(4,1)} %bitcast.6), calls=%async_computation.14 | async-start | bytes 3932160
Sparse Core Ops, SparseCore 0:
  11.5 138.9 reduce-scatter.7
  154.1 136.1 reduce-scatter.5
  293.8 136.1 reduce-scatter.3
  432.3 110.1 all-gather.7
  544.8 110.1 all-gather.5
  657.3 110.1 all-gather.3
where the time goes:
time: 820 us
  waiting for transfers between devices  724 us (88%)
  local copies, waits for them, and re-layouts  45.9 us (6%)
  other arithmetic  35.6 us (4%)
  between operations  14.2 us (2%)
    reduce_scatter x3, waiting for transfers between devices, step(): lax.psum_scatter(t[0], 'dp', scatter_dimension=1, tiled=True)  397 us
    all_gather x3, waiting for transfers between devices, step(): whole = [lax.all_gather(one[0], 'dp', axis=1, tiled=True) for one in new]  326 us
    unnamed x15, local copies, waits for them, and re-layouts  45.9 us
    convert_element_type x3, other arithmetic, adamw(): return ((w - 0.02 * step).astype(jnp.bfloat16), m, v)  35.6 us
  transfers between devices with their start and end apart: 6, of which 6 were waited for; matrix products, arithmetic and copies ran while one was open for 4% of the time, Pallas kernels for 0%

commit v1 on v0

v1 whole, which is shorter than its diff:
```python
import functools

import jax
import jax.numpy as jnp
from jax import lax
from jax.experimental import pallas as pl
from jax.experimental.pallas import tpu as pltpu
from jax.sharding import PartitionSpec as P


BF, F32 = jnp.bfloat16, jnp.float32
ANY = pl.BlockSpec(memory_space=pl.ANY)
X, Y, CORE = 4, 2, 1
PARTS = 5
LANES = 640
ROWS = 16


class Weight:
    def __init__(self, rows, cols, first, gathered):
        self.block, self.part, self.cols, self.first, self.gathered = rows // 8, rows // 8 // PARTS, cols, first, gathered
        self.shape = 0 if cols == 1280 else 1


def step_kernel(weights, *refs):
    n = len(weights)
    steps = n * PARTS
    refs = list(refs)

    def take(count):
        out = refs[:count]
        del refs[:count]
        return out

    g, w, m, v = take(n), take(n), take(n), take(n)
    g_out = take(n)
    new = [take(1)[0] if k.gathered else take(2) for k in weights]
    from_core, from_x, from_y = take(2), take(2), take(2)
    in1, out1, in2, out2, in3, old_w, mv, g3, new3 = (take(2) for _ in range(9))
    core_send, core_recv, load1, send1, load2, send2, recv_x, recv_y, load3, save3, own_send, own_recv, hop_send, hop_recv, twin_send, twin_recv, twin2_send, twin2_recv = refs

    me = lax.axis_index("dp")

    def to(mask):
        return dict(device_id={"dp": me ^ mask}, device_id_type=pl.DeviceIdType.MESH)

    def which(t):
        wt = t // PARTS
        return wt, weights[wt], t % PARTS

    def rows(t, device):
        _, k, part = which(t)
        return pl.ds(pl.multiple_of(device * k.block + part * k.part, 16), k.part)

    def land(t):
        _, k, part = which(t)
        place = part if k.shape == 0 else t - PARTS * sum(1 for o in weights[: t // PARTS] if o.shape == 0)
        return k.shape, place

    def vector(k, units, body):
        down, across = k.part // ROWS, k.cols // LANES

        @pl.loop(0, units * down * across)
        def _(i):
            u = i // (down * across)
            j = i % (down * across)
            r = pl.multiple_of((j // across) * ROWS, ROWS)
            c = pl.multiple_of((j % across) * LANES, 128)
            body(u, (pl.ds(r, ROWS), pl.ds(c, LANES)))

    targets = (X ^ Y, X, Y, 0)

    def core_copy(t, q):
        wt, _, _ = which(t)
        s, place = land(t)
        return pltpu.make_async_remote_copy(
            g[wt].at[:, rows(t, me ^ CORE ^ targets[q])], from_core[s].at[place, q], core_send.at[t, q], core_recv.at[t, q], **to(CORE)
        )

    units1 = ((0, 0), (1, 0), (0, 1), (2, 1))

    def own1(t, u):
        wt, k, _ = which(t)
        q, layer = units1[u]
        return pltpu.make_async_copy(g[wt].at[layer, rows(t, me ^ targets[q])], in1[k.shape].at[t % 2, u, 0], load1.at[t % 2, u, 0])

    def twin1(t, u):
        s, place = land(t)
        q, layer = units1[u]
        return pltpu.make_async_copy(from_core[s].at[place, q, layer], in1[s].at[t % 2, u, 1], load1.at[t % 2, u, 1])

    def go1(t, u):
        s, place = land(t)
        mask, dst, sem = ((X, from_x, recv_x), (Y, from_y, recv_y))[u // 2]
        return pltpu.make_async_remote_copy(out1[s].at[t % 2, u], dst[s].at[place, u % 2], send1.at[t % 2, u], sem.at[t, u % 2], **to(mask))

    units2 = ((2, 0, from_x, recv_x, Y, from_y, recv_y), (1, 1, from_y, recv_y, X, from_x, recv_x))

    def loads2(t, u):
        wt, _, _ = which(t)
        s, place = land(t)
        q, layer, src = units2[u][:3]
        return [
            pltpu.make_async_copy(g[wt].at[layer, rows(t, me ^ targets[q])], in2[s].at[t % 2, u, 0], load2.at[t % 2, u, 0]),
            pltpu.make_async_copy(from_core[s].at[place, q, layer], in2[s].at[t % 2, u, 1], load2.at[t % 2, u, 1]),
            pltpu.make_async_copy(src[s].at[place, 0], in2[s].at[t % 2, u, 2], load2.at[t % 2, u, 2]),
        ]

    def go2(t, u):
        s, place = land(t)
        mask, dst, sem = units2[u][4:]
        return pltpu.make_async_remote_copy(out2[s].at[t % 2, u], dst[s].at[place, 2], send2.at[t % 2, u], sem.at[t, 2], **to(mask))

    def loads3(t, layer):
        wt, k, part = which(t)
        s, place = land(t)
        straight, summed = (from_x, from_y) if layer == 0 else (from_y, from_x)
        mine = pl.ds(part * k.part, k.part)
        slot = t % 2
        to_in = [g[wt].at[layer, rows(t, me)], from_core[s].at[place, 3, layer], straight[s].at[place, 1], summed[s].at[place, 2]]
        out = [pltpu.make_async_copy(r, in3[s].at[slot, layer, i], load3.at[slot, layer, i]) for i, r in enumerate(to_in)]
        out.append(pltpu.make_async_copy(w[wt].at[layer, rows(t, me)], old_w[s].at[slot, layer], load3.at[slot, layer, 4]))
        out.append(pltpu.make_async_copy(m[wt].at[layer, mine], mv[s].at[slot, layer, 0], load3.at[slot, layer, 5]))
        out.append(pltpu.make_async_copy(v[wt].at[layer, mine], mv[s].at[slot, layer, 1], load3.at[slot, layer, 6]))
        return out

    def saves3(t, layer):
        wt, k, part = which(t)
        s, slot = k.shape, t % 2
        mine = pl.ds(part * k.part, k.part)
        dst = new[wt].at[layer, rows(t, me)] if k.gathered else new[wt][layer].at[mine]
        return [
            pltpu.make_async_copy(g3[s].at[slot, layer], g_out[wt].at[layer, mine], save3.at[slot, layer, 0]),
            pltpu.make_async_copy(new3[s].at[slot, layer], dst, save3.at[slot, layer, 1]),
        ]

    masks = (X, Y, CORE)

    def own_copy(t, layer, i):
        wt, k, _ = which(t)
        return pltpu.make_async_remote_copy(
            new3[k.shape].at[t % 2, layer], new[wt].at[layer, rows(t, me)], own_send.at[t % 2, layer, i], own_recv.at[t, layer, i], **to(masks[i])
        )

    def pass_copy(t, layer, source, target, send, recv):
        wt, _, _ = which(t)
        place = new[wt].at[layer, rows(t, me ^ source)]
        return pltpu.make_async_remote_copy(place, place, send, recv, **to(target))

    def hop(t, layer):
        source, target = ((X, Y), (Y, X))[layer]
        return pass_copy(t, layer, source, target, hop_send.at[t, layer], hop_recv.at[t, layer])

    def twin(t, layer, i):
        return pass_copy(t, layer, masks[i], CORE, twin_send.at[t, layer, i], twin_recv.at[t, layer, i])

    def twin2(t, layer):
        return pass_copy(t, layer, X ^ Y, CORE, twin2_send.at[t, layer], twin2_recv.at[t, layer])

    def real(t):
        return 0 <= t < steps

    def gathered(t):
        return real(t) and which(t)[1].gathered

    for u in range(4):
        own1(0, u).start()
    barrier = pltpu.get_barrier_semaphore()
    for mask in masks:
        pl.semaphore_signal(barrier, inc=1, **to(mask))
    pl.semaphore_wait(barrier, 3)

    def start_core(t):
        for q in range(4):
            core_copy(t, q).start()

    def prepare1(t):
        for q in range(4):
            core_copy(t, q).wait_recv()
        for u in range(4):
            twin1(t, u).start()

    start_core(0)
    start_core(1)
    prepare1(0)
    for t in range(steps + 4):
        if real(t + 2):
            start_core(t + 2)
        if real(t):
            s, k = which(t)[1].shape, which(t)[1]
            slot = t % 2
            for u in range(4):
                own1(t, u).wait()
                twin1(t, u).wait()
            if t >= 2:
                for u in range(4):
                    go1(t - 2, u).wait_send()

            def sum1(u, at, s=s, slot=slot):
                out1[s][slot, u, *at] = (in1[s][slot, u, 0, *at].astype(F32) + in1[s][slot, u, 1, *at].astype(F32)).astype(BF)

            vector(k, 4, sum1)
            for u in (0, 2, 1, 3):
                go1(t, u).start()
        if real(t + 1):
            for u in range(4):
                own1(t + 1, u).start()
            prepare1(t + 1)
        a = t - 1
        if real(a):
            for u in range(2):
                first = go1(a, 2 * u)
                first.wait_recv()
                for c in loads2(a, u):
                    c.start()
        b = t - 2
        if real(b):
            for layer in range(2):
                (go1(b, 1) if layer == 0 else go1(b, 3)).wait_recv()
                go2(b, layer).wait_recv()
                for c in loads3(b, layer):
                    c.start()
        if real(a):
            s, k, slot = which(a)[1].shape, which(a)[1], a % 2
            for u in range(2):
                for c in loads2(a, u):
                    c.wait()
                if a >= 2:
                    go2(a - 2, u).wait_send()

            def sum2(u, at, s=s, slot=slot):
                out2[s][slot, u, *at] = (
                    in2[s][slot, u, 0, *at].astype(F32) + in2[s][slot, u, 1, *at].astype(F32) + in2[s][slot, u, 2, *at].astype(F32)
                ).astype(BF)

            vector(k, 2, sum2)
            for u in range(2):
                go2(a, u).start()
        if real(b):
            s, k, slot = which(b)[1].shape, which(b)[1], b % 2
            for layer in range(2):
                for c in loads3(b, layer):
                    c.wait()
                if b >= 2:
                    for c in saves3(b - 2, layer):
                        c.wait()
                    if gathered(b - 2):
                        for i in range(3):
                            own_copy(b - 2, layer, i).wait_send()

            def update(u, at, s=s, slot=slot):
                parts = [in3[s][slot, u, i, *at].astype(F32) for i in range(4)]
                total = (((parts[0] + parts[1]) + parts[2]) + parts[3]).astype(BF)
                g3[s][slot, u, *at] = total
                total = total.astype(F32)
                new_m = 0.9 * mv[s][slot, u, 0, *at] + 0.1 * total
                new_v = 0.95 * mv[s][slot, u, 1, *at] + 0.05 * total * total
                weight = old_w[s][slot, u, *at].astype(F32)
                new3[s][slot, u, *at] = (weight - 0.02 * (new_m * lax.rsqrt(new_v + 1e-8) + 0.1 * weight)).astype(BF)

            vector(k, 2, update)
            for layer in range(2):
                for c in saves3(b, layer):
                    c.start()
            if gathered(b):
                for layer, i in ((0, 0), (1, 1), (1, 0), (0, 1), (0, 2), (1, 2)):
                    own_copy(b, layer, i).start()
        c3 = t - 3
        if gathered(c3):
            for layer in range(2):
                own_copy(c3, layer, layer).wait_recv()
                hop(c3, layer).start()
                twin(c3, layer, layer).start()
            for layer in range(2):
                own_copy(c3, layer, 1 - layer).wait_recv()
                twin(c3, layer, 1 - layer).start()
        c4 = t - 4
        if gathered(c4):
            for layer in range(2):
                hop(c4, layer).wait_recv()
                twin2(c4, layer).start()

    for t in range(steps):
        for q in range(4):
            core_copy(t, q).wait_send()
    for t in range(steps - 2, steps):
        for u in range(4):
            go1(t, u).wait_send()
        for u in range(2):
            go2(t, u).wait_send()
            for c in saves3(t, u):
                c.wait()
            if gathered(t):
                for i in range(3):
                    own_copy(t, u, i).wait_send()
    for t in range(steps):
        if gathered(t):
            for layer in range(2):
                own_copy(t, layer, 2).wait_recv()
                hop(t, layer).wait_send()
                for i in range(2):
                    twin(t, layer, i).wait()
                twin2(t, layer).wait()


def reduce_and_step(g, w, m, v, gathered):
    weights, first = [], 0
    for one, whole in zip(w, gathered, strict=True):
        weights.append(Weight(one.shape[1], one.shape[2], first, whole))
        first += PARTS
    n, steps = len(w), first
    dims = {k.shape: (k.part, k.cols) for k in weights}
    held = {s: PARTS * sum(1 for k in weights if k.shape == s) for s in dims}
    pair = [dims[s] for s in (0, 1)]

    def hbm(*lead):
        return [jax.ShapeDtypeStruct((held[s], *lead, *dims[s]), BF) for s in (0, 1)]

    def vmem(*lead, dtype=BF):
        return [pltpu.VMEM((*lead, *d), dtype) for d in pair]

    blocks = [jax.ShapeDtypeStruct((2, k.block, k.cols), BF) for k in weights]
    out_shape = list(blocks)
    for k in weights:
        one = [jax.ShapeDtypeStruct((2, 8 * k.block, k.cols), BF)] if k.gathered else [jax.ShapeDtypeStruct((k.block, k.cols), BF)] * 2
        out_shape += one
    out_shape += hbm(4, 2) + hbm(3) + hbm(3)
    dma = pltpu.SemaphoreType.DMA
    outs = pl.pallas_call(
        functools.partial(step_kernel, weights),
        out_shape=out_shape,
        in_specs=[ANY] * (4 * n),
        out_specs=[ANY] * len(out_shape),
        scratch_shapes=[
            *vmem(2, 4, 2),
            *vmem(2, 4),
            *vmem(2, 2, 3),
            *vmem(2, 2),
            *vmem(2, 2, 4),
            *vmem(2, 2),
            *vmem(2, 2, 2, dtype=F32),
            *vmem(2, 2),
            *vmem(2, 2),
            dma((steps, 4)),
            dma((steps, 4)),
            dma((2, 4, 2)),
            dma((2, 4)),
            dma((2, 2, 3)),
            dma((2, 2)),
            dma((steps, 3)),
            dma((steps, 3)),
            dma((2, 2, 7)),
            dma((2, 2, 2)),
            dma((2, 2, 3)),
            dma((steps, 2, 3)),
            dma((steps, 2)),
            dma((steps, 2)),
            dma((steps, 2, 2)),
            dma((steps, 2, 2)),
            dma((steps, 2)),
            dma((steps, 2)),
        ],
        compiler_params=pltpu.CompilerParams(collective_id=0, has_side_effects=True, vmem_limit_bytes=60 << 20),
        cost_estimate=pl.CostEstimate(flops=10**9, bytes_accessed=4 * 10**8, transcendentals=10**7),
        name="reduce_and_step",
    )(*g, *w, *m, *v)
    rest = list(outs[n:])
    return outs[:n], [rest.pop(0) if k.gathered else (rest.pop(0), rest.pop(0)) for k in weights]


def cost(bytes_accessed, flops):
    return pl.CostEstimate(flops=flops, bytes_accessed=bytes_accessed, transcendentals=0)


def copied(x):
    layers, rows, cols = x.shape
    part, slots = rows // 8, 8
    pieces = [(layer, i) for layer in range(layers) for i in range(8)]

    def body(src, dst, held, sem_in, sem_out):
        def get(j):
            layer, i = pieces[j]
            return pltpu.make_async_copy(src.at[layer, pl.ds(i * part, part)], held.at[j % slots], sem_in.at[j % slots])

        def put(j):
            layer, i = pieces[j]
            return pltpu.make_async_copy(held.at[j % slots], dst.at[layer, pl.ds(i * part, part)], sem_out.at[j % slots])

        lag = slots // 2
        for j in range(len(pieces) + lag):
            if j < len(pieces):
                if j >= slots:
                    put(j - slots).wait()
                get(j).start()
            if j >= lag:
                get(j - lag).wait()
                put(j - lag).start()
        for j in range(len(pieces) - slots, len(pieces)):
            put(j).wait()

    return pl.pallas_call(
        body,
        out_shape=jax.ShapeDtypeStruct(x.shape, x.dtype),
        in_specs=[ANY],
        out_specs=ANY,
        scratch_shapes=[pltpu.VMEM((slots, part, cols), x.dtype), pltpu.SemaphoreType.DMA((slots,)), pltpu.SemaphoreType.DMA((slots,))],
        cost_estimate=cost(4 * x.size, 10**8),
        name="copied",
    )(x)


def placed(pieces, out, rows):
    n, cols = len(pieces), pieces[0][0].shape[-1]

    def body(*refs):
        src, (dst, held, sem) = refs[:n], refs[-3:]
        me = lax.axis_index("dp")
        gets = [pltpu.make_async_copy(src[i], held.at[i], sem.at[0, i]) for i in range(n)]
        puts = []
        for i, (_, layer, mask) in enumerate(pieces):
            to = pl.ds(pl.multiple_of((me ^ mask) * rows, 16), rows)
            puts.append(pltpu.make_async_copy(held.at[i], dst.at[layer, to], sem.at[1, i]))
        for c in gets:
            c.start()
        for a, b in zip(gets, puts, strict=True):
            a.wait()
            b.start()
        for c in puts:
            c.wait()

    args = [one[0] for one in pieces] + ([] if out is None else [out])
    return pl.pallas_call(
        body,
        out_shape=jax.ShapeDtypeStruct((2, rows * 8, cols), BF),
        in_specs=[ANY] * len(args),
        out_specs=ANY,
        input_output_aliases={} if out is None else {n: 0},
        scratch_shapes=[pltpu.VMEM((n, rows, cols), BF), pltpu.SemaphoreType.DMA((2, n))],
        cost_estimate=cost(4 * n * rows * cols, 10**7),
        name="placed",
    )(*args)


def moved(x, mask):
    return lax.ppermute(x, "dp", [(i, i ^ mask) for i in range(8)])


def moments(m, v, g):
    g = g.astype(F32)
    return 0.9 * m + 0.1 * g, 0.95 * v + 0.05 * g * g


def solution(mesh):
    def inner(*arrays):
        terms, weights, m, v = (arrays[i : i + 3] for i in (0, 3, 6, 9))
        order = (2, 0, 1)
        sums, new = reduce_and_step([terms[i][0] for i in order], [weights[i] for i in order], [m[i] for i in order], [v[i] for i in order], (False, True, True))
        sums = [sums[order.index(i)] for i in range(3)]
        (A, B), gate, up = new
        rows = A.shape[0]
        xA, yB, xB, yA = moved(A, X), moved(B, Y), moved(B, X), moved(A, Y)
        cA, cB = moved(A, CORE), moved(B, CORE)
        dA, dB = moved(xA, Y), moved(yB, X)
        gate = copied(gate)
        up = copied(up)
        down = placed([(A, 0, 0), (B, 1, 0), (cA, 0, CORE), (cB, 1, CORE)], None, rows)
        cxA, cyB, cxB, cyA = moved(xA, CORE), moved(yB, CORE), moved(xB, CORE), moved(yA, CORE)
        down = placed([(xA, 0, X), (xB, 1, X), (yA, 0, Y), (yB, 1, Y)], down, rows)
        down = placed([(cxA, 0, X + CORE), (cxB, 1, X + CORE), (cyA, 0, Y + CORE), (cyB, 1, Y + CORE)], down, rows)
        cdA, cdB = moved(dA, CORE), moved(dB, CORE)
        down = placed([(dA, 0, X + Y), (dB, 1, X + Y)], down, rows)
        down = placed([(cdA, 0, X + Y + CORE), (cdB, 1, X + Y + CORE)], down, rows)
        after = []
        for i in range(3):
            after.append(moments(m[i], v[i], sums[i]))
        return (gate, up, down, *(one[0] for one in after), *(one[1] for one in after))

    all_of, cut = P(None, None, None), P(None, "dp", None)
    return jax.shard_map(
        inner,
        mesh=mesh,
        in_specs=(P(("rep", "dp"), None, None, None),) * 3 + (all_of,) * 3 + (cut,) * 6,
        out_specs=(P("rep", None, None),) * 3 + (P("rep", "dp", None),) * 6,
        check_vma=False,
    )
```

time: 820 us -> 612 us (0.75)
  waiting for transfers between devices: 724 us -> 41.1 us
  Pallas kernels: 0 us -> 533 us
  local copies, waits for them, and re-layouts: 45.9 us -> 0.57 us
  between operations: 14.2 us -> 0.79 us
    pallas_call x0 -> x8, Pallas kernels: none -> 533 us  [the longest x1 481 us: reduce_and_step(): pl.pallas_call(functools.partial(step_kernel, weights), out_shape=out_sha...]
    reduce_scatter x3 -> x0, waiting for transfers between devices: 397 us -> none  [step(): lax.psum_scatter(t[0], 'dp', scatter_dimension=1, tiled=True)]
    all_gather x3 -> x0, waiting for transfers between devices: 326 us -> none  [step(): whole = [lax.all_gather(one[0], 'dp', axis=1, tiled=True) for one in new]]
    unnamed x15 -> x6, local copies, waits for them, and re-layouts: 45.9 us -> 0.57 us
    ppermute x0 -> x14, waiting for transfers between devices: none -> 41.1 us  [moved(): return lax.ppermute(x, 'dp', [(i, i ^ mask) for i in range(8)])]
    convert_element_type x3 -> x0, other arithmetic: 35.6 us -> none  [adamw(): return ((w - 0.02 * step).astype(jnp.bfloat16), m, v)]
    add x0 -> x2, other arithmetic: none -> 28.9 us  [moments(): return (0.9 * m + 0.1 * g, 0.95 * v + 0.05 * g * g)]
  transfers between devices with their start and end apart: 6 -> 14, of which waited for: 6 -> 4; matrix products, arithmetic and copies ran while one was open for 4% -> 5% of each run, Pallas kernels for 0% -> 8%
where the time goes in v1:
time: 612 us
  Pallas kernels  533 us (87%)
  waiting for transfers between devices  41.1 us (7%)
  other arithmetic  28.9 us (5%)
  starting transfers between devices  7.38 us (1%)
    pallas_call x1, Pallas kernels, reduce_and_step(): pl.pallas_call(functools.partial(step_kernel, weights), out_shape=out_sha...  481 us
    ppermute x14, waiting for transfers between devices, moved(): return lax.ppermute(x, 'dp', [(i, i ^ mask) for i in range(8)])  41.1 us
    pallas_call x2, Pallas kernels, copied(): pl.pallas_call(body, out_shape=jax.ShapeDtypeStruct(x.shape, x.dtype), in...  31.8 us
    add x2, other arithmetic, moments(): return (0.9 * m + 0.1 * g, 0.95 * v + 0.05 * g * g)  28.9 us
    pallas_call x5, Pallas kernels, placed(): pl.pallas_call(body, out_shape=jax.ShapeDtypeStruct((2, rows * 8, cols),...  20 us
  transfers between devices with their start and end apart: 14, of which 4 were waited for; matrix products, arithmetic and copies ran while one was open for 5% of the time, Pallas kernels for 8%

profile of v1, /device:TPU:0, one launch (start us, length us, event | category | flops | bytes accessed | tf_op | source)
XLA Modules:
  0.0 611.8 jit_solution(17963350353144408810)
XLA Ops:
  0.6 481.2 %reduce_and_step.1 = (bf16[2,560,1280]{2,1,0:T(8,128)(2,1)}, bf16[2,160,4480]{2,1,0:T(8,128)(2,1)}, bf16[2,160,4480]{2,1,0:T(8,128)(2,1)}, bf16[560,1280]{1,0:T(...) custom-call(bf16[2,4480,1280]{2,1,0:T(8,128)(2,1)} %bitcast.3, ...), custom_call_target="tpu_custom_call" | custom-call | flops 1000000000 | bytes 400000000 | tf_op jit(solution)/shard_map/reduce_and_step/pallas_call | solution.py:329
  481.9 1.1 collective-permute-start
  483.0 1.0 collective-permute-start.3
  483.9 0.8 collective-permute-start.7
  484.7 1.2 collective-permute-start.9
  485.9 15.9 %copied.2 = bf16[2,1280,4480]{2,1,0:T(8,128)(2,1)} custom-call(bf16[2,1280,4480]{2,1,0:T(8,128)(2,1)} %get-tuple-element.16.src), custom_call_target="tpu_custom_call" | custom-call | flops 100000000 | bytes 45875200 | tf_op jit(solution)/shard_map/copied/pallas_call | solution.py:401
  501.9 15.9 %copied.3 = bf16[2,1280,4480]{2,1,0:T(8,128)(2,1)} custom-call(bf16[2,1280,4480]{2,1,0:T(8,128)(2,1)} %get-tuple-element.17.src), custom_call_target="tpu_custom_call" | custom-call | flops 100000000 | bytes 45875200 | tf_op jit(solution)/shard_map/copied/pallas_call | solution.py:401
  517.8 0.5 collective-permute-start.13
  518.3 0.6 copy-done.2
  518.9 0.8 collective-permute-start.1
  519.7 26.9 %collective-permute-done.7.refs_1_ = bf16[560,1280]{1,0:T(8,128)(2,1)} collective-permute-done((bf16[560,1280]{1,0:T(8,128)(2,1)}, bf16[560,1280]{1,0:T(8,128)(2,1)}, u32[]{:S(2)}, u32[]{:S(2)}) %collective-permute-start.7) | collective-permute-done | bytes 1433632 | tf_op jit(solution)/shard_map/ppermute | solution.py:445
  546.6 1.7 collective-permute-done.9.refs_2_
  548.3 1.0 collective-permute-start.4
  549.2 18.4 %fusion.3 = (f32[2,160,4480]{2,1,0:T(8,128)}, f32[2,160,4480]{2,1,0:T(8,128)}, f32[2,160,4480]{2,1,0:T(8,128)}, f32[2,160,4480]{2,1,0:T(8,128)}) fusion(bf16[2,160,4480]{2,1,0:T(8,128)(2,1)} %get-tuple-element.20, f32[2,160,4480]{2,1,0:T(8,128)} %refs_10_.1, f32[2,160,4480]{2,1,0:T(8,128)} %refs_7_.1, bf16[2,160,4480]{2,1,0:T(8,128)(2,1)} %get-tuple-element.21, ...), kind=kLoop, calls=%fused_computation.9 | loop fusion | flops 22937600 | bytes 51609600 | tf_op jit(solution)/shard_map/add | solution.py:450
  567.7 0.5 collective-permute-start.8
  568.2 9.8 %collective-permute-done.1.refs_0_ = bf16[560,1280]{1,0:T(8,128)(2,1)S(1)} collective-permute-done((bf16[560,1280]{1,0:T(8,128)(2,1)}, bf16[560,1280]{1,0:T(8,128)(2,1)S(1)}, u32[]{:S(2)}, u32[]{:S(2)}) %collective-permute-start.1) | collective-permute-done | bytes 1433632 | tf_op jit(solution)/shard_map/ppermute | solution.py:445
  578.0 2.7 collective-permute-done.4.refs_1_
  580.8 0.5 collective-permute-start.5
  581.3 10.4 %fusion.5 = (f32[2,560,1280]{2,1,0:T(8,128)}, f32[2,560,1280]{2,1,0:T(8,128)}) fusion(bf16[2,560,1280]{2,1,0:T(8,128)(2,1)S(1)} %copy-done, f32[2,560,1280]{2,1,0:T(8,128)} %refs_9_.1, f32[2,560,1280]{2,1,0:T(8,128)} %refs_6_.1), kind=kLoop, calls=%fused_computation.11 | loop fusion | flops 11468800 | bytes 25804800 | tf_op jit(solution)/shard_map/add | solution.py:450
  591.7 4.7 placed.5.refs_4_
  596.4 4.7 placed.6.refs_4_
  601.1 4.7 placed.7.refs_2_
  605.8 3.0 placed.8.refs_2_
  608.8 3.0 placed.9
  (20 shorter events, 0.1 us)
Async XLA Ops:
  481.9 35.9 %collective-permute-start = (bf16[560,1280]{1,0:T(8,128)(2,1)}, bf16[560,1280]{1,0:T(8,128)(2,1)S(1)}, u32[]{:S(2)}, u32[]{:S(2)}) collective-permute-start(bf16[560,1280]{1,0:T(8,128)(2,1)} %get-tuple-element.18.refs_0_), channel_id=1, source_target_pairs={{0,4},{1,5},{2,6},{3,7},{4,0},{5,1},{6,2},{7,3}} | collective-permute-start | bytes 4300808 | tf_op jit(solution)/shard_map/ppermute | solution.py:445
  483.0 36.0 %collective-permute-start.3 = (bf16[560,1280]{1,0:T(8,128)(2,1)}, bf16[560,1280]{1,0:T(8,128)(2,1)}, u32[]{:S(2)}, u32[]{:S(2)}) collective-permute-start(bf16[560,1280]{1,0:T(8,128)(2,1)} %get-tuple-element.19.refs_1_), channel_id=1, source_target_pairs={{0,2},{1,3},{2,0},{3,1},{4,6},{5,7},{6,4},{7,5}} | collective-permute-start | bytes 4300808 | tf_op jit(solution)/shard_map/ppermute | solution.py:445
  483.9 62.7 %collective-permute-start.7 = (bf16[560,1280]{1,0:T(8,128)(2,1)}, bf16[560,1280]{1,0:T(8,128)(2,1)}, u32[]{:S(2)}, u32[]{:S(2)}) collective-permute-start(bf16[560,1280]{1,0:T(8,128)(2,1)} %get-tuple-element.19.refs_1_), channel_id=1, source_target_pairs={{0,4},{1,5},{2,6},{3,7},{4,0},{5,1},{6,2},{7,3}} | collective-permute-start | bytes 4300808 | tf_op jit(solution)/shard_map/ppermute | solution.py:445
  484.7 63.6 %collective-permute-start.9 = (bf16[560,1280]{1,0:T(8,128)(2,1)}, bf16[560,1280]{1,0:T(8,128)(2,1)}, u32[]{:S(2)}, u32[]{:S(2)}) collective-permute-start(bf16[560,1280]{1,0:T(8,128)(2,1)} %get-tuple-element.18.refs_0_), channel_id=1, source_target_pairs={{0,2},{1,3},{2,0},{3,1},{4,6},{5,7},{6,4},{7,5}} | collective-permute-start | bytes 4300808 | tf_op jit(solution)/shard_map/ppermute | solution.py:445
  485.9 81.7 %collective-permute-start.12 = (bf16[560,1280]{1,0:T(8,128)(2,1)}, bf16[560,1280]{1,0:T(8,128)(2,1)}, u32[]{:S(2)}, u32[]{:S(2)}) collective-permute-start(bf16[560,1280]{1,0:T(8,128)(2,1)} %get-tuple-element.18.refs_0_), channel_id=1, source_target_pairs={{0,1},{1,0},{2,3},{3,2},{4,5},{5,4},{6,7},{7,6}} | collective-permute-start | bytes 4300808 | tf_op jit(solution)/shard_map/ppermute | solution.py:445
  517.8 1.1 copy-start.2
  517.8 49.9 %collective-permute-start.13 = (bf16[560,1280]{1,0:T(8,128)(2,1)}, bf16[560,1280]{1,0:T(8,128)(2,1)}, u32[]{:S(2)}, u32[]{:S(2)}) collective-permute-start(bf16[560,1280]{1,0:T(8,128)(2,1)} %get-tuple-element.19.refs_1_), channel_id=1, source_target_pairs={{0,1},{1,0},{2,3},{3,2},{4,5},{5,4},{6,7},{7,6}} | collective-permute-start | bytes 4300808 | tf_op jit(solution)/shard_map/ppermute | solution.py:445
  518.9 59.1 %collective-permute-start.1 = (bf16[560,1280]{1,0:T(8,128)(2,1)}, bf16[560,1280]{1,0:T(8,128)(2,1)S(1)}, u32[]{:S(2)}, u32[]{:S(2)}) collective-permute-start(bf16[560,1280]{1,0:T(8,128)(2,1)} %copy-done.2), channel_id=1, source_target_pairs={{0,2},{1,3},{2,0},{3,1},{4,6},{5,7},{6,4},{7,5}} | collective-permute-start | bytes 4300808 | tf_op jit(solution)/shard_map/ppermute | solution.py:445
  546.6 34.2 %collective-permute-start.6 = (bf16[560,1280]{1,0:T(8,128)(2,1)}, bf16[560,1280]{1,0:T(8,128)(2,1)}, u32[]{:S(2)}, u32[]{:S(2)}) collective-permute-start(bf16[560,1280]{1,0:T(8,128)(2,1)} %copy-done.2), channel_id=1, source_target_pairs={{0,1},{1,0},{2,3},{3,2},{4,5},{5,4},{6,7},{7,6}} | collective-permute-start | bytes 4300808 | tf_op jit(solution)/shard_map/ppermute | solution.py:445
  548.3 32.5 %collective-permute-start.4 = (bf16[560,1280]{1,0:T(8,128)(2,1)}, bf16[560,1280]{1,0:T(8,128)(2,1)}, u32[]{:S(2)}, u32[]{:S(2)}) collective-permute-start(bf16[560,1280]{1,0:T(8,128)(2,1)} %collective-permute-done.3.refs_3_), channel_id=1, source_target_pairs={{0,4},{1,5},{2,6},{3,7},{4,0},{5,1},{6,2},{7,3}} | collective-permute-start | bytes 4300808 | tf_op jit(solution)/shard_map/ppermute | solution.py:445
  549.2 32.0 %copy-start = (bf16[2,560,1280]{2,1,0:T(8,128)(2,1)S(1)}, bf16[2,560,1280]{2,1,0:T(8,128)(2,1)}, u32[]{:S(2)}) copy-start(bf16[2,560,1280]{2,1,0:T(8,128)(2,1)} %get-tuple-element.22) | copy-start | bytes 8601604
  567.7 33.4 %collective-permute-start.11 = (bf16[560,1280]{1,0:T(8,128)(2,1)}, bf16[560,1280]{1,0:T(8,128)(2,1)}, u32[]{:S(2)}, u32[]{:S(2)}) collective-permute-start(bf16[560,1280]{1,0:T(8,128)(2,1)} %collective-permute-done.3.refs_3_), channel_id=1, source_target_pairs={{0,1},{1,0},{2,3},{3,2},{4,5},{5,4},{6,7},{7,6}} | collective-permute-start | bytes 4300808 | tf_op jit(solution)/shard_map/ppermute | solution.py:445
  567.7 33.3 %collective-permute-start.8 = (bf16[560,1280]{1,0:T(8,128)(2,1)}, bf16[560,1280]{1,0:T(8,128)(2,1)}, u32[]{:S(2)}, u32[]{:S(2)}) collective-permute-start(bf16[560,1280]{1,0:T(8,128)(2,1)} %collective-permute-done.7.refs_1_), channel_id=1, source_target_pairs={{0,1},{1,0},{2,3},{3,2},{4,5},{5,4},{6,7},{7,6}} | collective-permute-start | bytes 4300808 | tf_op jit(solution)/shard_map/ppermute | solution.py:445
  578.0 13.7 %copy-start.1 = (bf16[560,1280]{1,0:T(8,128)(2,1)}, bf16[560,1280]{1,0:T(8,128)(2,1)S(1)}, u32[]{:S(2)}) copy-start(bf16[560,1280]{1,0:T(8,128)(2,1)S(1)} %collective-permute-done.1.refs_0_) | copy-start | bytes 4300804
  578.0 23.1 %collective-permute-start.10 = (bf16[560,1280]{1,0:T(8,128)(2,1)}, bf16[560,1280]{1,0:T(8,128)(2,1)}, u32[]{:S(2)}, u32[]{:S(2)}) collective-permute-start(bf16[560,1280]{1,0:T(8,128)(2,1)} %collective-permute-done.9.refs_2_), channel_id=1, source_target_pairs={{0,1},{1,0},{2,3},{3,2},{4,5},{5,4},{6,7},{7,6}} | collective-permute-start | bytes 4300808 | tf_op jit(solution)/shard_map/ppermute | solution.py:445
  580.8 28.0 %collective-permute-start.2 = (bf16[560,1280]{1,0:T(8,128)(2,1)S(1)}, bf16[560,1280]{1,0:T(8,128)(2,1)}, u32[]{:S(2)}, u32[]{:S(2)}) collective-permute-start(bf16[560,1280]{1,0:T(8,128)(2,1)S(1)} %collective-permute-done.1.refs_0_), channel_id=1, source_target_pairs={{0,1},{1,0},{2,3},{3,2},{4,5},{5,4},{6,7},{7,6}} | collective-permute-start | bytes 4300808 | tf_op jit(solution)/shard_map/ppermute | solution.py:445
  580.8 28.0 %collective-permute-start.5 = (bf16[560,1280]{1,0:T(8,128)(2,1)}, bf16[560,1280]{1,0:T(8,128)(2,1)}, u32[]{:S(2)}, u32[]{:S(2)}) collective-permute-start(bf16[560,1280]{1,0:T(8,128)(2,1)} %collective-permute-done.4.refs_1_), channel_id=1, source_target_pairs={{0,1},{1,0},{2,3},{3,2},{4,5},{5,4},{6,7},{7,6}} | collective-permute-start | bytes 4300808 | tf_op jit(solution)/shard_map/ppermute | solution.py:445

commit v2 on v1

v2 whole, which is shorter than its diff:
```python
import functools

import jax
import jax.numpy as jnp
from jax import lax
from jax.experimental import pallas as pl
from jax.experimental.pallas import tpu as pltpu
from jax.sharding import PartitionSpec as P


BF, F32 = jnp.bfloat16, jnp.float32
ANY = pl.BlockSpec(memory_space=pl.ANY)
X, Y, CORE = 4, 2, 1
LANES = 640
ROWS = 16


class Weight:
    def __init__(self, w, cuts, split=None):
        self.block, self.cols, self.cuts, self.split = w.shape[1] // 8, w.shape[2], cuts, split
        self.gathered = split is None
        self.shape = 0 if self.cols == 1280 else 1
        assert sum(cuts) == self.block and (split is None or split in [sum(cuts[:i]) for i in range(len(cuts))])


def step_kernel(weights, *refs):
    n = len(weights)
    plan = [(i, sum(k.cuts[:j]), rows) for i, k in enumerate(weights) for j, rows in enumerate(k.cuts)]
    steps = len(plan)
    refs = list(refs)

    def take(count):
        out = refs[:count]
        del refs[:count]
        return out

    g, w, m, v = take(n), take(n), take(n), take(n)
    g_out = take(n)
    new = [take(1)[0] if k.gathered else take(8) for k in weights]
    from_core, from_x, from_y = take(n), take(n), take(n)
    in1, out1, in2, out2, in3, old_w, mv, g3, new3 = (take(2) for _ in range(9))
    core_send, core_recv, load1, send1, load2, send2, recv_x, recv_y, load3, save3, own_send, own_recv, hop_send, hop_recv, twin_send, twin_recv, twin2_send, twin2_recv = refs

    me = lax.axis_index("dp")

    def to(mask):
        return dict(device_id={"dp": me ^ mask}, device_id_type=pl.DeviceIdType.MESH)

    def which(t):
        wt, first, size = plan[t]
        return wt, weights[wt].shape, first, size

    def rows(t, device):
        wt, _, first, size = which(t)
        return pl.ds(pl.multiple_of(device * weights[wt].block + first, 16), size)

    def mine(t):
        return pl.ds(plan[t][1], plan[t][2])

    def held(t, ref, *at):
        ref = ref[which(t)[1]]
        return ref.at[(t % ref.shape[0], *at, pl.ds(0, plan[t][2]))]

    def vector(t, units, body):
        wt, s, _, size = which(t)
        down, across = size // ROWS, weights[wt].cols // LANES

        @pl.loop(0, units * down * across)
        def _(i):
            u = i // (down * across)
            j = i % (down * across)
            r = pl.multiple_of((j // across) * ROWS, ROWS)
            c = pl.multiple_of((j % across) * LANES, 128)
            body(s, t % 2, u, (pl.ds(r, ROWS), pl.ds(c, LANES)))

    targets = (X ^ Y, X, Y, 0)

    def core_copy(t, q):
        wt = plan[t][0]
        return pltpu.make_async_remote_copy(
            g[wt].at[:, rows(t, me ^ CORE ^ targets[q])], from_core[wt].at[q, :, mine(t)], core_send.at[t, q], core_recv.at[t, q], **to(CORE)
        )

    units1 = ((0, 0), (1, 0), (0, 1), (2, 1))

    def own1(t, u):
        q, layer = units1[u]
        return pltpu.make_async_copy(g[plan[t][0]].at[layer, rows(t, me ^ targets[q])], held(t, in1, u, 0), load1.at[t % 2, u, 0])

    def twin1(t, u):
        q, layer = units1[u]
        return pltpu.make_async_copy(from_core[plan[t][0]].at[q, layer, mine(t)], held(t, in1, u, 1), load1.at[t % 2, u, 1])

    def go1(t, u):
        mask, dst, sem = ((X, from_x, recv_x), (Y, from_y, recv_y))[u // 2]
        return pltpu.make_async_remote_copy(held(t, out1, u), dst[plan[t][0]].at[u % 2, mine(t)], send1.at[t % 2, u], sem.at[t, u % 2], **to(mask))

    units2 = ((2, 0, from_x, Y, from_y, recv_y), (1, 1, from_y, X, from_x, recv_x))

    def loads2(t, u):
        wt = plan[t][0]
        q, layer, src = units2[u][:3]
        sources = (g[wt].at[layer, rows(t, me ^ targets[q])], from_core[wt].at[q, layer, mine(t)], src[wt].at[0, mine(t)])
        return [pltpu.make_async_copy(r, held(t, in2, u, i), load2.at[t % 2, u, i]) for i, r in enumerate(sources)]

    def go2(t, u):
        mask, dst, sem = units2[u][3:]
        return pltpu.make_async_remote_copy(held(t, out2, u), dst[plan[t][0]].at[2, mine(t)], send2.at[t % 2, u], sem.at[t, 2], **to(mask))

    def loads3(t, layer):
        wt = plan[t][0]
        straight, summed = (from_x, from_y) if layer == 0 else (from_y, from_x)
        moves = [
            (g[wt].at[layer, rows(t, me)], held(t, in3, layer, 0)),
            (from_core[wt].at[3, layer, mine(t)], held(t, in3, layer, 1)),
            (w[wt].at[layer, rows(t, me)], held(t, old_w, layer)),
            (m[wt].at[layer, mine(t)], held(t, mv, layer, 0)),
            (v[wt].at[layer, mine(t)], held(t, mv, layer, 1)),
            (straight[wt].at[1, mine(t)], held(t, in3, layer, 2)),
            (summed[wt].at[2, mine(t)], held(t, in3, layer, 3)),
        ]
        return [pltpu.make_async_copy(a, b, load3.at[t % 2, layer, i]) for i, (a, b) in enumerate(moves)]

    def piece(t, layer):
        wt, _, first, _ = which(t)
        k = weights[wt]
        return (new[wt][2 + 2 * layer], first) if first < k.split else (new[wt][3 + 2 * layer], first - k.split)

    def saves3(t, layer):
        wt, _, _, size = which(t)
        places = [g_out[wt].at[layer, mine(t)]]
        if weights[wt].gathered:
            places.append(new[wt].at[layer, rows(t, me)])
        else:
            ref, at = piece(t, layer)
            places += [new[wt][layer].at[mine(t)], ref.at[pl.ds(at, size)]]
        return [
            pltpu.make_async_copy(held(t, g3 if i == 0 else new3, layer), place, save3.at[t % 2, layer, i]) for i, place in enumerate(places)
        ]

    masks = (X, Y, CORE)

    def own_copy(t, layer, i):
        wt = plan[t][0]
        dst = new[wt].at[layer, rows(t, me)] if weights[wt].gathered else new[wt][6 + layer].at[mine(t)]
        return pltpu.make_async_remote_copy(held(t, new3, layer), dst, own_send.at[t % 2, layer, i], own_recv.at[t, layer, i], **to(masks[i]))

    def neighbours(t):
        return range(3) if gathered(t) else (2,)

    def pass_copy(t, layer, source, target, send, recv):
        place = new[plan[t][0]].at[layer, rows(t, me ^ source)]
        return pltpu.make_async_remote_copy(place, place, send, recv, **to(target))

    def hop(t, layer):
        source, target = ((X, Y), (Y, X))[layer]
        return pass_copy(t, layer, source, target, hop_send.at[t, layer], hop_recv.at[t, layer])

    def twin(t, layer, i):
        return pass_copy(t, layer, masks[i], CORE, twin_send.at[t, layer, i], twin_recv.at[t, layer, i])

    def twin2(t, layer):
        return pass_copy(t, layer, X ^ Y, CORE, twin2_send.at[t, layer], twin2_recv.at[t, layer])

    def real(t):
        return 0 <= t < steps

    def gathered(t):
        return real(t) and weights[plan[t][0]].gathered

    for u in range(4):
        own1(0, u).start()
    barrier = pltpu.get_barrier_semaphore()
    for mask in masks:
        pl.semaphore_signal(barrier, inc=1, **to(mask))
    pl.semaphore_wait(barrier, 3)

    def start_core(t):
        for q in range(4):
            core_copy(t, q).start()

    def prepare1(t):
        for q in range(4):
            core_copy(t, q).wait_recv()
        for u in range(4):
            twin1(t, u).start()

    start_core(0)
    start_core(1)
    prepare1(0)
    for t in range(steps + 4):
        if real(t + 2):
            start_core(t + 2)
        if real(t):
            for u in range(4):
                own1(t, u).wait()
                twin1(t, u).wait()
            if t >= 2:
                for u in range(4):
                    go1(t - 2, u).wait_send()

            def sum1(s, slot, u, at):
                out1[s][slot, u, *at] = (in1[s][0, u, 0, *at].astype(F32) + in1[s][0, u, 1, *at].astype(F32)).astype(BF)

            vector(t, 4, sum1)
            for u in (0, 2, 1, 3):
                go1(t, u).start()
        if real(t + 1):
            for u in range(4):
                own1(t + 1, u).start()
            prepare1(t + 1)
        a = t - 1
        if real(a):
            for u in range(2):
                for c in loads2(a, u)[:2]:
                    c.start()
            for u in range(2):
                go1(a, 2 * u).wait_recv()
                loads2(a, u)[2].start()
            for u in range(2):
                for c in loads2(a, u):
                    c.wait()
                if a >= 2:
                    go2(a - 2, u).wait_send()

            def sum2(s, slot, u, at):
                out2[s][slot, u, *at] = (
                    in2[s][0, u, 0, *at].astype(F32) + in2[s][0, u, 1, *at].astype(F32) + in2[s][0, u, 2, *at].astype(F32)
                ).astype(BF)

            vector(a, 2, sum2)
            for u in range(2):
                go2(a, u).start()
        b = t - 2
        if real(b):
            for layer in range(2):
                for c in loads3(b, layer)[:5]:
                    c.start()
            for layer in range(2):
                go1(b, 1 + 2 * layer).wait_recv()
                go2(b, layer).wait_recv()
                for c in loads3(b, layer)[5:]:
                    c.start()
            for layer in range(2):
                for c in loads3(b, layer):
                    c.wait()
                if b >= 2:
                    for c in saves3(b - 2, layer):
                        c.wait()
                    for i in neighbours(b - 2):
                        own_copy(b - 2, layer, i).wait_send()

            def update(s, slot, u, at):
                parts = [in3[s][0, u, i, *at].astype(F32) for i in range(4)]
                total = (((parts[0] + parts[1]) + parts[2]) + parts[3]).astype(BF)
                g3[s][slot, u, *at] = total
                total = total.astype(F32)
                new_m = 0.9 * mv[s][0, u, 0, *at] + 0.1 * total
                new_v = 0.95 * mv[s][0, u, 1, *at] + 0.05 * total * total
                weight = old_w[s][0, u, *at].astype(F32)
                new3[s][slot, u, *at] = (weight - 0.02 * (new_m * lax.rsqrt(new_v + 1e-8) + 0.1 * weight)).astype(BF)

            vector(b, 2, update)
            if gathered(b):
                for layer, i in ((0, 0), (1, 1), (1, 0), (0, 1)):
                    own_copy(b, layer, i).start()
            for layer in range(2):
                own_copy(b, layer, 2).start()
                for c in saves3(b, layer):
                    c.start()
        c3 = t - 3
        if gathered(c3):
            for layer in range(2):
                own_copy(c3, layer, layer).wait_recv()
                hop(c3, layer).start()
                twin(c3, layer, layer).start()
            for layer in range(2):
                own_copy(c3, layer, 1 - layer).wait_recv()
                twin(c3, layer, 1 - layer).start()
        c4 = t - 4
        if gathered(c4):
            for layer in range(2):
                hop(c4, layer).wait_recv()
                twin2(c4, layer).start()

    for t in range(steps):
        for q in range(4):
            core_copy(t, q).wait_send()
    for t in range(steps - 2, steps):
        for u in range(4):
            go1(t, u).wait_send()
        for u in range(2):
            go2(t, u).wait_send()
            for c in saves3(t, u):
                c.wait()
            for i in neighbours(t):
                own_copy(t, u, i).wait_send()
    for t in range(steps):
        for layer in range(2):
            own_copy(t, layer, 2).wait_recv()
            if gathered(t):
                hop(t, layer).wait_send()
                for i in range(2):
                    twin(t, layer, i).wait()
                twin2(t, layer).wait()


def reduce_and_step(g, w, m, v, cuts, split):
    weights = [Weight(one, cut, split if i == 0 else None) for i, (one, cut) in enumerate(zip(w, cuts, strict=True))]
    n, steps = len(w), sum(len(cut) for cut in cuts)
    pair = [max((max(k.cuts), k.cols) for k in weights if k.shape == s) for s in (0, 1)]

    def hbm(*lead):
        return [jax.ShapeDtypeStruct((*lead, k.block, k.cols), BF) for k in weights]

    def vmem(*lead, dtype=BF):
        return [pltpu.VMEM((*lead, *d), dtype) for d in pair]

    out_shape = hbm(2)
    for k in weights:
        sizes = (k.block, k.block, k.split, k.block - k.split, k.split, k.block - k.split, k.block, k.block) if k.split else ()
        out_shape += [jax.ShapeDtypeStruct((size, k.cols), BF) for size in sizes] or [jax.ShapeDtypeStruct((2, 8 * k.block, k.cols), BF)]
    out_shape += hbm(4, 2) + hbm(3) + hbm(3)
    dma = pltpu.SemaphoreType.DMA
    outs = pl.pallas_call(
        functools.partial(step_kernel, weights),
        out_shape=out_shape,
        in_specs=[ANY] * (4 * n),
        out_specs=[ANY] * len(out_shape),
        scratch_shapes=[
            *vmem(1, 4, 2),
            *vmem(2, 4),
            *vmem(1, 2, 3),
            *vmem(2, 2),
            *vmem(1, 2, 4),
            *vmem(1, 2),
            *vmem(1, 2, 2, dtype=F32),
            *vmem(2, 2),
            *vmem(2, 2),
            dma((steps, 4)),
            dma((steps, 4)),
            dma((2, 4, 2)),
            dma((2, 4)),
            dma((2, 2, 3)),
            dma((2, 2)),
            dma((steps, 3)),
            dma((steps, 3)),
            dma((2, 2, 7)),
            dma((2, 2, 3)),
            dma((2, 2, 3)),
            dma((steps, 2, 3)),
            dma((steps, 2)),
            dma((steps, 2)),
            dma((steps, 2, 2)),
            dma((steps, 2, 2)),
            dma((steps, 2)),
            dma((steps, 2)),
        ],
        compiler_params=pltpu.CompilerParams(collective_id=0, has_side_effects=True, vmem_limit_bytes=60 << 20),
        cost_estimate=pl.CostEstimate(flops=10**9, bytes_accessed=4 * 10**8, transcendentals=10**7),
        name="reduce_and_step",
    )(*g, *w, *m, *v)
    return outs[:n], outs[n : n + 8], outs[n + 8 : 2 * n + 7]


def cost(bytes_accessed, flops):
    return pl.CostEstimate(flops=flops, bytes_accessed=bytes_accessed, transcendentals=0)


def copied(x):
    layers, rows, cols = x.shape
    part, slots = rows // 8, 8
    pieces = [(layer, i) for layer in range(layers) for i in range(8)]

    def body(src, dst, held, sem_in, sem_out):
        def get(j):
            layer, i = pieces[j]
            return pltpu.make_async_copy(src.at[layer, pl.ds(i * part, part)], held.at[j % slots], sem_in.at[j % slots])

        def put(j):
            layer, i = pieces[j]
            return pltpu.make_async_copy(held.at[j % slots], dst.at[layer, pl.ds(i * part, part)], sem_out.at[j % slots])

        lag = slots // 2
        for j in range(len(pieces) + lag):
            if j < len(pieces):
                if j >= slots:
                    put(j - slots).wait()
                get(j).start()
            if j >= lag:
                get(j - lag).wait()
                put(j - lag).start()
        for j in range(len(pieces) - slots, len(pieces)):
            put(j).wait()

    return pl.pallas_call(
        body,
        out_shape=jax.ShapeDtypeStruct(x.shape, x.dtype),
        in_specs=[ANY],
        out_specs=ANY,
        scratch_shapes=[pltpu.VMEM((slots, part, cols), x.dtype), pltpu.SemaphoreType.DMA((slots,)), pltpu.SemaphoreType.DMA((slots,))],
        cost_estimate=cost(4 * x.size, 10**8),
        compiler_params=pltpu.CompilerParams(vmem_limit_bytes=16 << 20),
        name="copied",
    )(x)


def placed(pieces, out, block, near=True):
    n, cols = len(pieces), pieces[0][0].shape[-1]

    def body(*refs):
        src, (dst, *held, sem) = refs[:n], refs[n if out is None else n + 1 :]
        me = lax.axis_index("dp")
        if not near:
            gets = [pltpu.make_async_copy(a, b, sem.at[n + i]) for i, (a, b) in enumerate(zip(src, held, strict=True))]
            for c in gets:
                c.start()
            src = held
        puts = []
        for i, (one, layer, mask, first) in enumerate(pieces):
            to = pl.ds(pl.multiple_of((me ^ mask) * block + first, 16), one.shape[0])
            puts.append(pltpu.make_async_copy(src[i], dst.at[layer, to], sem.at[i]))
            if not near:
                gets[i].wait()
            puts[i].start()
        for c in puts:
            c.wait()

    args = [one[0] for one in pieces] + ([] if out is None else [out])
    scratch = [] if near else [pltpu.VMEM(one[0].shape, BF) for one in pieces]
    return pl.pallas_call(
        body,
        out_shape=jax.ShapeDtypeStruct((2, block * 8, cols), BF),
        in_specs=[pl.BlockSpec(memory_space=pltpu.VMEM) if near else ANY] * n + [ANY] * (len(args) - n),
        out_specs=ANY,
        input_output_aliases={} if out is None else {n: 0},
        scratch_shapes=[*scratch, pltpu.SemaphoreType.DMA((2 * n,))],
        cost_estimate=cost(4 * sum(one[0].size for one in pieces), 10**7),
        compiler_params=pltpu.CompilerParams(vmem_limit_bytes=8 << 20),
        name="placed",
    )(*args)


def moved(x, mask):
    return lax.ppermute(x, "dp", [(i, i ^ mask) for i in range(8)])


def moments(m, v, g):
    g = g.astype(F32)
    return 0.9 * m + 0.1 * g, 0.95 * v + 0.05 * g * g


CUTS = ((16, 48, 96, 128, 144, 128), (80, 80), (64, 48, 32, 16))
SPLIT = 432


def solution(mesh):
    def inner(*arrays):
        terms, weights, m, v = (arrays[i : i + 3] for i in (0, 3, 6, 9))
        order = (2, 0, 1)
        sums, mine, (gate, up) = reduce_and_step(
            [terms[i][0] for i in order], [weights[i] for i in order], [m[i] for i in order], [v[i] for i in order], CUTS, SPLIT
        )
        sums = [sums[order.index(i)] for i in range(3)]
        A, B, A0, A1, B0, B1, cA, cB = mine
        rows = A.shape[0]
        xA0, yB0, xA1, yB1 = moved(A0, X), moved(B0, Y), moved(A1, X), moved(B1, Y)
        xB, yA = moved(B, X), moved(A, Y)
        dA0, dB0, dA1, dB1 = moved(xA0, Y), moved(yB0, X), moved(xA1, Y), moved(yB1, X)
        gate = copied(gate)
        up = copied(up)

        def place(i, down, *pieces):
            return placed(pieces, down, rows, near=i > 0)

        def twins(*pieces):
            return [(moved(x, CORE), layer, mask + CORE, first) for x, layer, mask, first in pieces]

        near = [(xA0, 0, X, 0), (yB0, 1, Y, 0), (xA1, 0, X, SPLIT), (yB1, 1, Y, SPLIT), (xB, 1, X, 0), (yA, 0, Y, 0)]
        far0, far1 = [(dA0, 0, X + Y, 0), (dB0, 1, X + Y, 0)], [(dA1, 0, X + Y, SPLIT), (dB1, 1, X + Y, SPLIT)]
        down = place(0, None, (A, 0, 0, 0), (B, 1, 0, 0), (cA, 0, CORE, 0), (cB, 1, CORE, 0))
        down = place(1, down, *near)
        down = place(2, down, *twins(*near))
        down = place(3, down, *far0)
        down = place(4, down, *twins(*far0))
        down = place(5, down, *far1)
        last = [(moved(x, CORE), layer, mask + CORE, first) for x, layer, mask, first in far1]
        down = place(6, down, *last)
        after = []
        for i in range(3):
            after.append(moments(m[i], v[i], sums[i]))
        return (gate, up, down, *(one[0] for one in after), *(one[1] for one in after))

    all_of, cut = P(None, None, None), P(None, "dp", None)
    return jax.shard_map(
        inner,
        mesh=mesh,
        in_specs=(P(("rep", "dp"), None, None, None),) * 3 + (all_of,) * 3 + (cut,) * 6,
        out_specs=(P("rep", None, None),) * 3 + (P("rep", "dp", None),) * 6,
        check_vma=False,
    )
```

time: 612 us -> 645 us (1.054)
  waiting for transfers between devices: 41.1 us -> 71.2 us
  Pallas kernels: 533 us -> 517 us
  local copies, waits for them, and re-layouts: 0.57 us -> 13.8 us
    ppermute x14 -> x20, waiting for transfers between devices: 41.1 us -> 71.2 us  [moved(): return lax.ppermute(x, 'dp', [(i, i ^ mask) for i in range(8)])]
    unnamed x6 -> x62, local copies, waits for them, and re-layouts: 0.57 us -> 13.8 us
    pallas_call x2, Pallas kernels: 31.8 us -> 19.5 us  [copied(): pl.pallas_call(body, out_shape=jax.ShapeDtypeStruct(x.shape, x.dtype), in...]
    pallas_call x5 -> x7, Pallas kernels: 20 us -> 21.5 us  [placed(): pl.pallas_call(body, out_shape=jax.ShapeDtypeStruct((2, block * 8, cols),...]
  transfers between devices with their start and end apart: 14 -> 20, of which waited for: 4 -> 6; matrix products, arithmetic and copies ran while one was open for 5% -> 5% of each run, Pallas kernels for 8% -> 6%
where the time goes in v2:
time: 645 us; the launch traced here: 644 us
  Pallas kernels  517 us (80%)
  waiting for transfers between devices  71.2 us (11%)
  other arithmetic  29.6 us (5%)
  local copies, waits for them, and re-layouts  13.8 us (2%)
  starting transfers between devices  11.9 us (2%)
    pallas_call x1, Pallas kernels, reduce_and_step(): pl.pallas_call(functools.partial(step_kernel, weights), out_shape=out_sha...  476 us
    ppermute x20, waiting for transfers between devices, moved(): return lax.ppermute(x, 'dp', [(i, i ^ mask) for i in range(8)])  71.2 us
    add x2, other arithmetic, moments(): return (0.9 * m + 0.1 * g, 0.95 * v + 0.05 * g * g)  29.6 us
    pallas_call x7, Pallas kernels, placed(): pl.pallas_call(body, out_shape=jax.ShapeDtypeStruct((2, block * 8, cols),...  21.5 us
    pallas_call x2, Pallas kernels, copied(): pl.pallas_call(body, out_shape=jax.ShapeDtypeStruct(x.shape, x.dtype), in...  19.5 us
    unnamed x62, local copies, waits for them, and re-layouts  13.8 us
  transfers between devices with their start and end apart: 20, of which 6 were waited for; matrix products, arithmetic and copies ran while one was open for 5% of the time, Pallas kernels for 6%

profile of v2, /device:TPU:0, one launch (start us, length us, event | category | flops | bytes accessed | tf_op | source)
XLA Modules:
  0.0 644.4 jit_solution(3120546700988106539)
XLA Ops:
  0.6 475.7 %reduce_and_step.1 = (bf16[2,560,1280]{2,1,0:T(8,128)(2,1)}, bf16[2,160,4480]{2,1,0:T(8,128)(2,1)}, bf16[2,160,4480]{2,1,0:T(8,128)(2,1)}, bf16[560,1280]{1,0:T(...) custom-call(bf16[2,4480,1280]{2,1,0:T(8,128)(2,1)} %bitcast.5, ...), custom_call_target="tpu_custom_call" | custom-call | flops 1000000000 | bytes 400000000 | tf_op jit(solution)/shard_map/reduce_and_step/pallas_call | solution.py:325
  476.4 1.1 collective-permute-start
  479.3 1.2 collective-permute-start.18
  480.5 6.7 %collective-permute-done.refs_2_ = bf16[128,1280]{1,0:T(8,128)(2,1)S(1)} collective-permute-done((bf16[128,1280]{1,0:T(8,128)(2,1)}, bf16[128,1280]{1,0:T(8,128)(2,1)S(1)}, u32[]{:S(2)}, u32[]{:S(2)}) %collective-permute-start) | collective-permute-done | bytes 327712 | tf_op jit(solution)/shard_map/ppermute | solution.py:445
  488.1 1.2 collective-permute-start.6
  489.2 1.1 collective-permute-start.9
  490.3 35.7 %collective-permute-done.1.refs_0_ = bf16[128,1280]{1,0:T(8,128)(2,1)S(1)} collective-permute-done((bf16[128,1280]{1,0:T(8,128)(2,1)S(1)}, bf16[128,1280]{1,0:T(8,128)(2,1)S(1)}, u32[]{:S(2)}, u32[]{:S(2)}) %collective-permute-start.1) | collective-permute-done | bytes 327712 | tf_op jit(solution)/shard_map/ppermute | solution.py:445
  527.0 21.1 %collective-permute-done.4.refs_1_ = bf16[128,1280]{1,0:T(8,128)(2,1)S(1)} collective-permute-done((bf16[128,1280]{1,0:T(8,128)(2,1)S(1)}, bf16[128,1280]{1,0:T(8,128)(2,1)S(1)}, u32[]{:S(2)}, u32[]{:S(2)}) %collective-permute-start.4) | collective-permute-done | bytes 327712 | tf_op jit(solution)/shard_map/ppermute | solution.py:445
  553.0 1.2 collective-permute-start.10
  554.7 18.3 %fusion.3 = (f32[2,160,4480]{2,1,0:T(8,128)}, f32[2,160,4480]{2,1,0:T(8,128)}, f32[2,160,4480]{2,1,0:T(8,128)}, f32[2,160,4480]{2,1,0:T(8,128)}) fusion(bf16[2,160,4480]{2,1,0:T(8,128)(2,1)} %get-tuple-element.32, f32[2,160,4480]{2,1,0:T(8,128)} %refs_10_.1, f32[2,160,4480]{2,1,0:T(8,128)} %refs_7_.1, bf16[2,160,4480]{2,1,0:T(8,128)(2,1)} %get-tuple-element.33, ...), kind=kLoop, calls=%fused_computation.9 | loop fusion | flops 22937600 | bytes 51609600 | tf_op jit(solution)/shard_map/add | solution.py:450
  573.0 5.0 collective-permute-done.7.refs_0_
  578.0 1.7 collective-permute-done.10.refs_1_
  580.3 1.1 copy-done.7
  581.9 11.3 %fusion.5 = (f32[2,560,1280]{2,1,0:T(8,128)}, f32[2,560,1280]{2,1,0:T(8,128)}) fusion(bf16[2,560,1280]{2,1,0:T(8,128)(2,1)} %get-tuple-element.34, f32[2,560,1280]{2,1,0:T(8,128)} %refs_9_.1, f32[2,560,1280]{2,1,0:T(8,128)} %refs_6_.1), kind=kLoop, calls=%fused_computation.11 | loop fusion | flops 11468800 | bytes 25804800 | tf_op jit(solution)/shard_map/add | solution.py:450
  593.2 1.4 copy-done.4
  594.6 3.9 placed.7.refs_6_
  598.5 8.3 %copy-done = bf16[2,1280,4480]{2,1,0:T(8,128)(2,1)S(1)} copy-done((bf16[2,1280,4480]{2,1,0:T(8,128)(2,1)S(1)}, bf16[2,1280,4480]{2,1,0:T(8,128)(2,1)}, u32[]{:S(2)}) %copy-start) | copy-done | bytes 22937624
  606.9 10.5 %copied.2 = bf16[2,1280,4480]{2,1,0:T(8,128)(2,1)} custom-call(bf16[2,1280,4480]{2,1,0:T(8,128)(2,1)S(1)} %copy-done), custom_call_target="tpu_custom_call" | custom-call | flops 100000000 | bytes 45875200 | tf_op jit(solution)/shard_map/copied/pallas_call | solution.py:396
  617.5 9.1 %copied.3 = bf16[2,1280,4480]{2,1,0:T(8,128)(2,1)} custom-call(bf16[2,1280,4480]{2,1,0:T(8,128)(2,1)S(1)} %bitcast.4), custom_call_target="tpu_custom_call" | custom-call | flops 100000000 | bytes 45875200 | tf_op jit(solution)/shard_map/copied/pallas_call | solution.py:396
  626.6 4.1 placed.8.refs_6_
  630.8 4.7 placed.9.refs_2_
  635.4 3.0 placed.10.refs_2_
  638.5 3.0 placed.11.refs_2_
  642.4 1.9 placed.13
  (91 shorter events, 11.1 us)
Async XLA Ops:
  476.4 10.8 %collective-permute-start = (bf16[128,1280]{1,0:T(8,128)(2,1)}, bf16[128,1280]{1,0:T(8,128)(2,1)S(1)}, u32[]{:S(2)}, u32[]{:S(2)}) collective-permute-start(bf16[128,1280]{1,0:T(8,128)(2,1)} %get-tuple-element.24), channel_id=1, source_target_pairs={{0,4},{1,5},{2,6},{3,7},{4,0},{5,1},{6,2},{7,3}} | collective-permute-start | bytes 983048 | tf_op jit(solution)/shard_map/ppermute | solution.py:445
  477.5 11.8 %collective-permute-start.3 = (bf16[128,1280]{1,0:T(8,128)(2,1)}, bf16[128,1280]{1,0:T(8,128)(2,1)S(1)}, u32[]{:S(2)}, u32[]{:S(2)}) collective-permute-start(bf16[128,1280]{1,0:T(8,128)(2,1)} %get-tuple-element.25), channel_id=1, source_target_pairs={{0,2},{1,3},{2,0},{3,1},{4,6},{5,7},{6,4},{7,5}} | collective-permute-start | bytes 983048 | tf_op jit(solution)/shard_map/ppermute | solution.py:445
  478.5 75.7 %collective-permute-start.16 = (bf16[560,1280]{1,0:T(8,128)(2,1)}, bf16[560,1280]{1,0:T(8,128)(2,1)S(1)}, u32[]{:S(2)}, u32[]{:S(2)}) collective-permute-start(bf16[560,1280]{1,0:T(8,128)(2,1)} %get-tuple-element.28.refs_1_), channel_id=1, source_target_pairs={{0,4},{1,5},{2,6},{3,7},{4,0},{5,1},{6,2},{7,3}} | collective-permute-start | bytes 4300808 | tf_op jit(solution)/shard_map/ppermute | solution.py:445
  479.3 75.0 %collective-permute-start.18 = (bf16[560,1280]{1,0:T(8,128)(2,1)}, bf16[560,1280]{1,0:T(8,128)(2,1)}, u32[]{:S(2)}, u32[]{:S(2)}) collective-permute-start(bf16[560,1280]{1,0:T(8,128)(2,1)} %get-tuple-element.29.refs_0_), channel_id=1, source_target_pairs={{0,2},{1,3},{2,0},{3,1},{4,6},{5,7},{6,4},{7,5}} | collective-permute-start | bytes 4300808 | tf_op jit(solution)/shard_map/ppermute | solution.py:445
  487.2 38.8 %collective-permute-start.1 = (bf16[128,1280]{1,0:T(8,128)(2,1)S(1)}, bf16[128,1280]{1,0:T(8,128)(2,1)S(1)}, u32[]{:S(2)}, u32[]{:S(2)}) collective-permute-start(bf16[128,1280]{1,0:T(8,128)(2,1)S(1)} %collective-permute-done.refs_2_), channel_id=1, source_target_pairs={{0,2},{1,3},{2,0},{3,1},{4,6},{5,7},{6,4},{7,5}} | collective-permute-start | bytes 983048 | tf_op jit(solution)/shard_map/ppermute | solution.py:445
  488.1 63.2 %collective-permute-start.6 = (bf16[432,1280]{1,0:T(8,128)(2,1)}, bf16[432,1280]{1,0:T(8,128)(2,1)S(1)}, u32[]{:S(2)}, u32[]{:S(2)}) collective-permute-start(bf16[432,1280]{1,0:T(8,128)(2,1)} %get-tuple-element.26), channel_id=1, source_target_pairs={{0,4},{1,5},{2,6},{3,7},{4,0},{5,1},{6,2},{7,3}} | collective-permute-start | bytes 3317768 | tf_op jit(solution)/shard_map/ppermute | solution.py:445
  489.2 63.7 %collective-permute-start.9 = (bf16[432,1280]{1,0:T(8,128)(2,1)}, bf16[432,1280]{1,0:T(8,128)(2,1)S(1)}, u32[]{:S(2)}, u32[]{:S(2)}) collective-permute-start(bf16[432,1280]{1,0:T(8,128)(2,1)} %get-tuple-element.27), channel_id=1, source_target_pairs={{0,2},{1,3},{2,0},{3,1},{4,6},{5,7},{6,4},{7,5}} | collective-permute-start | bytes 3317768 | tf_op jit(solution)/shard_map/ppermute | solution.py:445
  526.0 28.3 %copy-start.13 = (bf16[128,1280]{1,0:T(8,128)(2,1)}, bf16[128,1280]{1,0:T(8,128)(2,1)S(1)}, u32[]{:S(2)}) copy-start(bf16[128,1280]{1,0:T(8,128)(2,1)S(1)} %collective-permute-done.1.refs_0_) | copy-start | bytes 983044
  526.0 22.0 %collective-permute-start.4 = (bf16[128,1280]{1,0:T(8,128)(2,1)S(1)}, bf16[128,1280]{1,0:T(8,128)(2,1)S(1)}, u32[]{:S(2)}, u32[]{:S(2)}) collective-permute-start(bf16[128,1280]{1,0:T(8,128)(2,1)S(1)} %collective-permute-done.3.refs_3_), channel_id=1, source_target_pairs={{0,4},{1,5},{2,6},{3,7},{4,0},{5,1},{6,2},{7,3}} | collective-permute-start | bytes 983048 | tf_op jit(solution)/shard_map/ppermute | solution.py:445
  548.1 1.6 collective-permute-start.14
  550.4 1.7 collective-permute-start.15
  551.3 26.8 %collective-permute-start.7 = (bf16[432,1280]{1,0:T(8,128)(2,1)S(1)}, bf16[432,1280]{1,0:T(8,128)(2,1)}, u32[]{:S(2)}, u32[]{:S(2)}) collective-permute-start(bf16[432,1280]{1,0:T(8,128)(2,1)S(1)} %collective-permute-done.6.refs_0_), channel_id=1, source_target_pairs={{0,2},{1,3},{2,0},{3,1},{4,6},{5,7},{6,4},{7,5}} | collective-permute-start | bytes 3317768 | tf_op jit(solution)/shard_map/ppermute | solution.py:445
  552.9 26.9 %collective-permute-start.12 = (bf16[432,1280]{1,0:T(8,128)(2,1)S(1)}, bf16[432,1280]{1,0:T(8,128)(2,1)}, u32[]{:S(2)}, u32[]{:S(2)}) collective-permute-start(bf16[432,1280]{1,0:T(8,128)(2,1)S(1)} %collective-permute-done.6.refs_0_), channel_id=1, source_target_pairs={{0,1},{1,0},{2,3},{3,2},{4,5},{5,4},{6,7},{7,6}} | collective-permute-start | bytes 3317768 | tf_op jit(solution)/shard_map/ppermute | solution.py:445
  553.0 26.8 %collective-permute-start.10 = (bf16[432,1280]{1,0:T(8,128)(2,1)S(1)}, bf16[432,1280]{1,0:T(8,128)(2,1)}, u32[]{:S(2)}, u32[]{:S(2)}) collective-permute-start(bf16[432,1280]{1,0:T(8,128)(2,1)S(1)} %collective-permute-done.9.refs_1_), channel_id=1, source_target_pairs={{0,4},{1,5},{2,6},{3,7},{4,0},{5,1},{6,2},{7,3}} | collective-permute-start | bytes 3317768 | tf_op jit(solution)/shard_map/ppermute | solution.py:445
  554.1 26.1 %collective-permute-start.13 = (bf16[432,1280]{1,0:T(8,128)(2,1)S(1)}, bf16[432,1280]{1,0:T(8,128)(2,1)}, u32[]{:S(2)}, u32[]{:S(2)}) collective-permute-start(bf16[432,1280]{1,0:T(8,128)(2,1)S(1)} %collective-permute-done.9.refs_1_), channel_id=1, source_target_pairs={{0,1},{1,0},{2,3},{3,2},{4,5},{5,4},{6,7},{7,6}} | collective-permute-start | bytes 3317768 | tf_op jit(solution)/shard_map/ppermute | solution.py:445
  554.3 26.0 %collective-permute-start.17 = (bf16[560,1280]{1,0:T(8,128)(2,1)S(1)}, bf16[560,1280]{1,0:T(8,128)(2,1)S(1)}, u32[]{:S(2)}, u32[]{:S(2)}) collective-permute-start(bf16[560,1280]{1,0:T(8,128)(2,1)S(1)} %collective-permute-done.16.refs_4_), channel_id=1, source_target_pairs={{0,1},{1,0},{2,3},{3,2},{4,5},{5,4},{6,7},{7,6}} | collective-permute-start | bytes 4300808 | tf_op jit(solution)/shard_map/ppermute | solution.py:445
  578.0 64.4 %collective-permute-start.2 = (bf16[128,1280]{1,0:T(8,128)(2,1)}, bf16[128,1280]{1,0:T(8,128)(2,1)}, u32[]{:S(2)}, u32[]{:S(2)}) collective-permute-start(bf16[128,1280]{1,0:T(8,128)(2,1)} %copy-done.13), channel_id=1, source_target_pairs={{0,1},{1,0},{2,3},{3,2},{4,5},{5,4},{6,7},{7,6}} | collective-permute-start | bytes 983048 | tf_op jit(solution)/shard_map/ppermute | solution.py:445
  579.8 62.6 %collective-permute-start.5 = (bf16[128,1280]{1,0:T(8,128)(2,1)}, bf16[128,1280]{1,0:T(8,128)(2,1)}, u32[]{:S(2)}, u32[]{:S(2)}) collective-permute-start(bf16[128,1280]{1,0:T(8,128)(2,1)} %copy-done.17), channel_id=1, source_target_pairs={{0,1},{1,0},{2,3},{3,2},{4,5},{5,4},{6,7},{7,6}} | collective-permute-start | bytes 983048 | tf_op jit(solution)/shard_map/ppermute | solution.py:445
  579.8 51.0 %collective-permute-start.19 = (bf16[560,1280]{1,0:T(8,128)(2,1)}, bf16[560,1280]{1,0:T(8,128)(2,1)}, u32[]{:S(2)}, u32[]{:S(2)}) collective-permute-start(bf16[560,1280]{1,0:T(8,128)(2,1)} %collective-permute-done.18.refs_5_), channel_id=1, source_target_pairs={{0,1},{1,0},{2,3},{3,2},{4,5},{5,4},{6,7},{7,6}} | collective-permute-start | bytes 4300808 | tf_op jit(solution)/shard_map/ppermute | solution.py:445
  580.3 58.2 %collective-permute-start.8 = (bf16[432,1280]{1,0:T(8,128)(2,1)}, bf16[432,1280]{1,0:T(8,128)(2,1)}, u32[]{:S(2)}, u32[]{:S(2)}) collective-permute-start(bf16[432,1280]{1,0:T(8,128)(2,1)} %collective-permute-done.7.refs_0_), channel_id=1, source_target_pairs={{0,1},{1,0},{2,3},{3,2},{4,5},{5,4},{6,7},{7,6}} | collective-permute-start | bytes 3317768 | tf_op jit(solution)/shard_map/ppermute | solution.py:445
  581.4 57.0 %collective-permute-start.11 = (bf16[432,1280]{1,0:T(8,128)(2,1)}, bf16[432,1280]{1,0:T(8,128)(2,1)}, u32[]{:S(2)}, u32[]{:S(2)}) collective-permute-start(bf16[432,1280]{1,0:T(8,128)(2,1)} %collective-permute-done.10.refs_1_), channel_id=1, source_target_pairs={{0,1},{1,0},{2,3},{3,2},{4,5},{5,4},{6,7},{7,6}} | collective-permute-start | bytes 3317768 | tf_op jit(solution)/shard_map/ppermute | solution.py:445
  594.6 22.8 %slice-start = ((s8[22937600]{0:T(1024)(128)(4,1)}), s8[4194304]{0:T(1024)(128)(4,1)S(1)}, s32[]{:S(2)}) async-start(s8[22937600]{0:T(1024)(128)(4,1)} %bitcast.3), calls=%async_computation | async-start | bytes 8388608
  594.6 22.8 %slice-start.1 = ((s8[22937600]{0:T(1024)(128)(4,1)}), s8[4194304]{0:T(1024)(128)(4,1)S(1)}, s32[]{:S(2)}) async-start(s8[22937600]{0:T(1024)(128)(4,1)} %bitcast.3), calls=%async_computation.1 | async-start | bytes 8388608
  594.6 22.8 %slice-start.2 = ((s8[22937600]{0:T(1024)(128)(4,1)}), s8[4194304]{0:T(1024)(128)(4,1)S(1)}, s32[]{:S(2)}) async-start(s8[22937600]{0:T(1024)(128)(4,1)} %bitcast.3), calls=%async_computation.2 | async-start | bytes 8388608
  (27 other events, 210.4 us)

commit v3 on v2

--- a/solution.py
+++ b/solution.py
@@ -13,6 +13,7 @@
 X, Y, CORE = 4, 2, 1
 LANES = 640
 ROWS = 16
+RING = 6
 
 
 class Weight:
@@ -37,9 +38,10 @@
     g, w, m, v = take(n), take(n), take(n), take(n)
     g_out = take(n)
     new = [take(1)[0] if k.gathered else take(8) for k in weights]
+    late = take(2)
     from_core, from_x, from_y = take(n), take(n), take(n)
     in1, out1, in2, out2, in3, old_w, mv, g3, new3 = (take(2) for _ in range(9))
-    core_send, core_recv, load1, send1, load2, send2, recv_x, recv_y, load3, save3, own_send, own_recv, hop_send, hop_recv, twin_send, twin_recv, twin2_send, twin2_recv = refs
+    core_send, core_recv, soon_send, soon_recv, load1, send1, load2, send2, recv_x, recv_y, load3, save3, own_send, own_recv, hop_send, hop_recv, twin_send, twin_recv, twin2_send, twin2_recv = refs
 
     me = lax.axis_index("dp")
 
@@ -75,25 +77,47 @@
 
     targets = (X ^ Y, X, Y, 0)
 
-    def core_copy(t, q):
-        wt = plan[t][0]
-        return pltpu.make_async_remote_copy(
-            g[wt].at[:, rows(t, me ^ CORE ^ targets[q])], from_core[wt].at[q, :, mine(t)], core_send.at[t, q], core_recv.at[t, q], **to(CORE)
-        )
+    def core_copies(t):
+        for q in range(4):
+            if t == 0 and q == 0:
+                continue
+            at = (1 if q == 1 else 0) if t == 0 and q in (1, 2) else slice(None)
+            yield pltpu.make_async_remote_copy(
+                g[plan[t][0]].at[at, rows(t, me ^ CORE ^ targets[q])],
+                from_core[plan[t][0]].at[q, at, mine(t)],
+                core_send.at[t % RING, q] if t else soon_send.at[4 + q],
+                core_recv.at[t % RING, q] if t else soon_recv.at[4 + q],
+                **to(CORE),
+            )
 
     units1 = ((0, 0), (1, 0), (0, 1), (2, 1))
 
     def own1(t, u):
         q, layer = units1[u]
-        return pltpu.make_async_copy(g[plan[t][0]].at[layer, rows(t, me ^ targets[q])], held(t, in1, u, 0), load1.at[t % 2, u, 0])
+        return pltpu.make_async_copy(g[plan[t][0]].at[layer, rows(t, me ^ targets[q])], held(t, in1, u, 0), load1.at[u, 0])
 
     def twin1(t, u):
         q, layer = units1[u]
-        return pltpu.make_async_copy(from_core[plan[t][0]].at[q, layer, mine(t)], held(t, in1, u, 1), load1.at[t % 2, u, 1])
+        return pltpu.make_async_copy(from_core[plan[t][0]].at[q, layer, mine(t)], held(t, in1, u, 1), load1.at[u, 1])
+
+    def soon(u):
+        q, layer = units1[u]
+        return pltpu.make_async_remote_copy(
+            g[plan[0][0]].at[layer, rows(0, me ^ CORE ^ targets[q])], held(0, in1, u, 1), soon_send.at[u], soon_recv.at[u], **to(CORE)
+        )
+
+    def merged(t):
+        return 3 <= t < steps - 2
+
+    def order1(t):
+        return (0, 2) if merged(t) else (0, 2, 1, 3)
 
     def go1(t, u):
         mask, dst, sem = ((X, from_x, recv_x), (Y, from_y, recv_y))[u // 2]
-        return pltpu.make_async_remote_copy(held(t, out1, u), dst[plan[t][0]].at[u % 2, mine(t)], send1.at[t % 2, u], sem.at[t, u % 2], **to(mask))
+        count = 2 if merged(t) else 1
+        return pltpu.make_async_remote_copy(
+            held(t, out1, pl.ds(u, count)), dst[plan[t][0]].at[pl.ds(u % 2, count), mine(t)], send1.at[t % 2, u], sem.at[t % RING, u % 2], **to(mask)
+        )
 
     units2 = ((2, 0, from_x, Y, from_y, recv_y), (1, 1, from_y, X, from_x, recv_x))
 
@@ -101,11 +125,11 @@
         wt = plan[t][0]
         q, layer, src = units2[u][:3]
         sources = (g[wt].at[layer, rows(t, me ^ targets[q])], from_core[wt].at[q, layer, mine(t)], src[wt].at[0, mine(t)])
-        return [pltpu.make_async_copy(r, held(t, in2, u, i), load2.at[t % 2, u, i]) for i, r in enumerate(sources)]
+        return [pltpu.make_async_copy(r, held(t, in2, u, i), load2.at[u, i]) for i, r in enumerate(sources)]
 
     def go2(t, u):
         mask, dst, sem = units2[u][3:]
-        return pltpu.make_async_remote_copy(held(t, out2, u), dst[plan[t][0]].at[2, mine(t)], send2.at[t % 2, u], sem.at[t, 2], **to(mask))
+        return pltpu.make_async_remote_copy(held(t, out2, u), dst[plan[t][0]].at[2, mine(t)], send2.at[t % 2, u], sem.at[t % RING, 2], **to(mask))
 
     def loads3(t, layer):
         wt = plan[t][0]
@@ -119,7 +143,7 @@
             (straight[wt].at[1, mine(t)], held(t, in3, layer, 2)),
             (summed[wt].at[2, mine(t)], held(t, in3, layer, 3)),
         ]
-        return [pltpu.make_async_copy(a, b, load3.at[t % 2, layer, i]) for i, (a, b) in enumerate(moves)]
+        return [pltpu.make_async_copy(a, b, load3.at[layer, i]) for i, (a, b) in enumerate(moves)]
 
     def piece(t, layer):
         wt, _, first, _ = which(t)
@@ -140,27 +164,39 @@
 
     masks = (X, Y, CORE)
 
+    def layers(t):
+        return (pl.ds(0, 2),) if merged(t) and gathered(t) else (0, 1)
+
+    def number(layer):
+        return layer if isinstance(layer, int) else 0
+
     def own_copy(t, layer, i):
         wt = plan[t][0]
         dst = new[wt].at[layer, rows(t, me)] if weights[wt].gathered else new[wt][6 + layer].at[mine(t)]
-        return pltpu.make_async_remote_copy(held(t, new3, layer), dst, own_send.at[t % 2, layer, i], own_recv.at[t, layer, i], **to(masks[i]))
-
-    def neighbours(t):
-        return range(3) if gathered(t) else (2,)
-
-    def pass_copy(t, layer, source, target, send, recv):
+        k = number(layer)
+        return pltpu.make_async_remote_copy(held(t, new3, layer), dst, own_send.at[t % 2, k, i], own_recv.at[t % RING, k, i], **to(masks[i]))
+
+    def own_copies(t):
+        if not gathered(t):
+            return [own_copy(t, layer, 2) for layer in layers(t)]
+        if merged(t):
+            return [own_copy(t, layer, i) for layer in layers(t) for i in range(3)]
+        return [own_copy(t, layer, i) for layer, i in ((0, 0), (1, 1), (1, 0), (0, 1), (0, 2), (1, 2))]
+
+    def pass_copy(t, layer, source, target, send, recv, dst=None):
         place = new[plan[t][0]].at[layer, rows(t, me ^ source)]
-        return pltpu.make_async_remote_copy(place, place, send, recv, **to(target))
+        return pltpu.make_async_remote_copy(place, place if dst is None else dst, send, recv, **to(target))
 
     def hop(t, layer):
         source, target = ((X, Y), (Y, X))[layer]
-        return pass_copy(t, layer, source, target, hop_send.at[t, layer], hop_recv.at[t, layer])
+        return pass_copy(t, layer, source, target, hop_send.at[t % RING, layer], hop_recv.at[t % RING, layer], late[layer] if t == steps - 1 else None)
 
     def twin(t, layer, i):
-        return pass_copy(t, layer, masks[i], CORE, twin_send.at[t, layer, i], twin_recv.at[t, layer, i])
+        k = number(layer)
+        return pass_copy(t, layer, masks[i], CORE, twin_send.at[t % RING, k, i], twin_recv.at[t % RING, k, i])
 
     def twin2(t, layer):
-        return pass_copy(t, layer, X ^ Y, CORE, twin2_send.at[t, layer], twin2_recv.at[t, layer])
+        return pass_copy(t, layer, X ^ Y, CORE, twin2_send.at[t % RING, layer], twin2_recv.at[t % RING, layer])
 
     def real(t):
         return 0 <= t < steps
@@ -176,34 +212,41 @@
     pl.semaphore_wait(barrier, 3)
 
     def start_core(t):
-        for q in range(4):
-            core_copy(t, q).start()
+        for c in core_copies(t):
+            c.start()
 
     def prepare1(t):
-        for q in range(4):
-            core_copy(t, q).wait_recv()
+        for c in core_copies(t):
+            c.wait_recv()
         for u in range(4):
             twin1(t, u).start()
 
+    for u in range(4):
+        soon(u).start()
     start_core(0)
     start_core(1)
-    prepare1(0)
-    for t in range(steps + 4):
+    for t in range(steps + 5):
         if real(t + 2):
+            if t + 2 - RING >= 1:
+                for c in core_copies(t + 2 - RING):
+                    c.wait_send()
             start_core(t + 2)
         if real(t):
             for u in range(4):
                 own1(t, u).wait()
-                twin1(t, u).wait()
+                if t == 0:
+                    soon(u).wait_recv()
+                else:
+                    twin1(t, u).wait()
             if t >= 2:
-                for u in range(4):
+                for u in order1(t - 2):
                     go1(t - 2, u).wait_send()
 
             def sum1(s, slot, u, at):
                 out1[s][slot, u, *at] = (in1[s][0, u, 0, *at].astype(F32) + in1[s][0, u, 1, *at].astype(F32)).astype(BF)
 
             vector(t, 4, sum1)
-            for u in (0, 2, 1, 3):
+            for u in order1(t):
                 go1(t, u).start()
         if real(t + 1):
             for u in range(4):
@@ -211,6 +254,9 @@
             prepare1(t + 1)
         a = t - 1
         if real(a):
+            if a == 0:
+                for c in core_copies(0):
+                    c.wait_recv()
             for u in range(2):
                 for c in loads2(a, u)[:2]:
                     c.start()
@@ -237,7 +283,8 @@
                 for c in loads3(b, layer)[:5]:
                     c.start()
             for layer in range(2):
-                go1(b, 1 + 2 * layer).wait_recv()
+                if not merged(b):
+                    go1(b, 1 + 2 * layer).wait_recv()
                 go2(b, layer).wait_recv()
                 for c in loads3(b, layer)[5:]:
                     c.start()
@@ -247,8 +294,10 @@
                 if b >= 2:
                     for c in saves3(b - 2, layer):
                         c.wait()
-                    for i in neighbours(b - 2):
-                        own_copy(b - 2, layer, i).wait_send()
+
+            if b >= 2:
+                for c in own_copies(b - 2):
+                    c.wait_send()
 
             def update(s, slot, u, at):
                 parts = [in3[s][0, u, i, *at].astype(F32) for i in range(4)]
@@ -261,53 +310,68 @@
                 new3[s][slot, u, *at] = (weight - 0.02 * (new_m * lax.rsqrt(new_v + 1e-8) + 0.1 * weight)).astype(BF)
 
             vector(b, 2, update)
-            if gathered(b):
-                for layer, i in ((0, 0), (1, 1), (1, 0), (0, 1)):
-                    own_copy(b, layer, i).start()
+            for c in own_copies(b):
+                c.start()
             for layer in range(2):
-                own_copy(b, layer, 2).start()
                 for c in saves3(b, layer):
                     c.start()
         c3 = t - 3
         if gathered(c3):
-            for layer in range(2):
-                own_copy(c3, layer, layer).wait_recv()
-                hop(c3, layer).start()
-                twin(c3, layer, layer).start()
-            for layer in range(2):
-                own_copy(c3, layer, 1 - layer).wait_recv()
-                twin(c3, layer, 1 - layer).start()
+            if merged(c3):
+                for i in range(2):
+                    own_copy(c3, layers(c3)[0], i).wait_recv()
+                for layer in range(2):
+                    hop(c3, layer).start()
+                for i in range(2):
+                    twin(c3, layers(c3)[0], i).start()
+            else:
+                for layer in range(2):
+                    own_copy(c3, layer, layer).wait_recv()
+                    hop(c3, layer).start()
+                    twin(c3, layer, layer).start()
+                for layer in range(2):
+                    own_copy(c3, layer, 1 - layer).wait_recv()
+                    twin(c3, layer, 1 - layer).start()
         c4 = t - 4
         if gathered(c4):
             for layer in range(2):
                 hop(c4, layer).wait_recv()
-                twin2(c4, layer).start()
-
-    for t in range(steps):
-        for q in range(4):
-            core_copy(t, q).wait_send()
+                if c4 < steps - 1:
+                    twin2(c4, layer).start()
+
+        if real(c4):
+            for layer in layers(c4):
+                own_copy(c4, layer, 2).wait_recv()
+        c5 = t - 5
+        if real(c5):
+            if gathered(c5):
+                for layer in layers(c5):
+                    for i in range(2):
+                        twin(c5, layer, i).wait()
+                for layer in range(2):
+                    hop(c5, layer).wait_send()
+                    if c5 < steps - 1:
+                        twin2(c5, layer).wait()
+
+    for u in range(4):
+        soon(u).wait_send()
+    for t in (0, *range(max(1, steps - RING), steps)):
+        for c in core_copies(t):
+            c.wait_send()
     for t in range(steps - 2, steps):
-        for u in range(4):
+        for u in order1(t):
             go1(t, u).wait_send()
         for u in range(2):
             go2(t, u).wait_send()
             for c in saves3(t, u):
                 c.wait()
-            for i in neighbours(t):
-                own_copy(t, u, i).wait_send()
-    for t in range(steps):
-        for layer in range(2):
-            own_copy(t, layer, 2).wait_recv()
-            if gathered(t):
-                hop(t, layer).wait_send()
-                for i in range(2):
-                    twin(t, layer, i).wait()
-                twin2(t, layer).wait()
+        for c in own_copies(t):
+            c.wait_send()
 
 
 def reduce_and_step(g, w, m, v, cuts, split):
     weights = [Weight(one, cut, split if i == 0 else None) for i, (one, cut) in enumerate(zip(w, cuts, strict=True))]
-    n, steps = len(w), sum(len(cut) for cut in cuts)
+    n = len(w)
     pair = [max((max(k.cuts), k.cols) for k in weights if k.shape == s) for s in (0, 1)]
 
     def hbm(*lead):
@@ -320,6 +384,7 @@
     for k in weights:
         sizes = (k.block, k.block, k.split, k.block - k.split, k.split, k.block - k.split, k.block, k.block) if k.split else ()
         out_shape += [jax.ShapeDtypeStruct((size, k.cols), BF) for size in sizes] or [jax.ShapeDtypeStruct((2, 8 * k.block, k.cols), BF)]
+    out_shape += [jax.ShapeDtypeStruct((weights[-1].cuts[-1], weights[-1].cols), BF)] * 2
     out_shape += hbm(4, 2) + hbm(3) + hbm(3)
     dma = pltpu.SemaphoreType.DMA
     outs = pl.pallas_call(
@@ -337,30 +402,32 @@
             *vmem(1, 2, 2, dtype=F32),
             *vmem(2, 2),
             *vmem(2, 2),
-            dma((steps, 4)),
-            dma((steps, 4)),
-            dma((2, 4, 2)),
+            dma((RING, 4)),
+            dma((RING, 4)),
+            dma((8,)),
+            dma((8,)),
+            dma((4, 2)),
             dma((2, 4)),
-            dma((2, 2, 3)),
+            dma((2, 3)),
             dma((2, 2)),
-            dma((steps, 3)),
-            dma((steps, 3)),
-            dma((2, 2, 7)),
+            dma((RING, 3)),
+            dma((RING, 3)),
+            dma((2, 7)),
             dma((2, 2, 3)),
             dma((2, 2, 3)),
-            dma((steps, 2, 3)),
-            dma((steps, 2)),
-            dma((steps, 2)),
-            dma((steps, 2, 2)),
-            dma((steps, 2, 2)),
-            dma((steps, 2)),
-            dma((steps, 2)),
+            dma((RING, 2, 3)),
+            dma((RING, 2)),
+            dma((RING, 2)),
+            dma((RING, 2, 2)),
+            dma((RING, 2, 2)),
+            dma((RING, 2)),
+            dma((RING, 2)),
         ],
         compiler_params=pltpu.CompilerParams(collective_id=0, has_side_effects=True, vmem_limit_bytes=60 << 20),
         cost_estimate=pl.CostEstimate(flops=10**9, bytes_accessed=4 * 10**8, transcendentals=10**7),
         name="reduce_and_step",
     )(*g, *w, *m, *v)
-    return outs[:n], outs[n : n + 8], outs[n + 8 : 2 * n + 7]
+    return outs[:n], outs[n : n + 8], outs[n + 8 : 2 * n + 7], outs[2 * n + 7 : 2 * n + 9]
 
 
 def cost(bytes_accessed, flops):
@@ -450,7 +517,7 @@
     return 0.9 * m + 0.1 * g, 0.95 * v + 0.05 * g * g
 
 
-CUTS = ((16, 48, 96, 128, 144, 128), (80, 80), (64, 48, 32, 16))
+CUTS = ((32, 64, 96, 112, 128, 128), (80, 80), (80, 48, 32))
 SPLIT = 432
 
 
@@ -458,7 +525,7 @@
     def inner(*arrays):
         terms, weights, m, v = (arrays[i : i + 3] for i in (0, 3, 6, 9))
         order = (2, 0, 1)
-        sums, mine, (gate, up) = reduce_and_step(
+        sums, mine, (gate, up), late = reduce_and_step(
             [terms[i][0] for i in order], [weights[i] for i in order], [m[i] for i in order], [v[i] for i in order], CUTS, SPLIT
         )
         sums = [sums[order.index(i)] for i in range(3)]
@@ -470,14 +537,17 @@
         gate = copied(gate)
         up = copied(up)
 
-        def place(i, down, *pieces):
-            return placed(pieces, down, rows, near=i > 0)
+        def place(i, whole, *pieces, block=rows):
+            return placed(pieces, whole, block, near=i > 0)
 
         def twins(*pieces):
             return [(moved(x, CORE), layer, mask + CORE, first) for x, layer, mask, first in pieces]
 
         near = [(xA0, 0, X, 0), (yB0, 1, Y, 0), (xA1, 0, X, SPLIT), (yB1, 1, Y, SPLIT), (xB, 1, X, 0), (yA, 0, Y, 0)]
         far0, far1 = [(dA0, 0, X + Y, 0), (dB0, 1, X + Y, 0)], [(dA1, 0, X + Y, SPLIT), (dB1, 1, X + Y, SPLIT)]
+        block = up.shape[1] // 8
+        far = [(x, layer, X + Y, block - CUTS[2][-1]) for layer, x in enumerate(late)]
+        up = place(7, up, *far, *twins(*far), block=block)
         down = place(0, None, (A, 0, 0, 0), (B, 1, 0, 0), (cA, 0, CORE, 0), (cB, 1, CORE, 0))
         down = place(1, down, *near)
         down = place(2, down, *twins(*near))

time: 645 us -> 644 us (level)
    unnamed x62 -> x74, local copies, waits for them, and re-layouts: 13.8 us -> 16.7 us
    ppermute x20 -> x22, waiting for transfers between devices: 71.2 us -> 70 us  [moved(): return lax.ppermute(x, 'dp', [(i, i ^ mask) for i in range(8)])]
    pallas_call x7 -> x8, Pallas kernels: 21.5 us -> 22.6 us  [placed(): pl.pallas_call(body, out_shape=jax.ShapeDtypeStruct((2, block * 8, cols),...]
  transfers between devices with their start and end apart: 20 -> 22, of which waited for: 6 -> 6; matrix products, arithmetic and copies ran while one was open for 5% -> 5% of each run, Pallas kernels for 6% -> 6%
where the time goes in v3:
time: 644 us; the launch traced here: 643 us
  Pallas kernels  514 us (80%)
  waiting for transfers between devices  70 us (11%)
  other arithmetic  29.6 us (5%)
  local copies, waits for them, and re-layouts  16.7 us (3%)
  starting transfers between devices  12.1 us (2%)
    pallas_call x1, Pallas kernels, reduce_and_step(): pl.pallas_call(functools.partial(step_kernel, weights), out_shape=out_sha...  472 us
    ppermute x22, waiting for transfers between devices, moved(): return lax.ppermute(x, 'dp', [(i, i ^ mask) for i in range(8)])  70 us
    add x2, other arithmetic, moments(): return (0.9 * m + 0.1 * g, 0.95 * v + 0.05 * g * g)  29.6 us
    pallas_call x8, Pallas kernels, placed(): pl.pallas_call(body, out_shape=jax.ShapeDtypeStruct((2, block * 8, cols),...  22.6 us
    pallas_call x2, Pallas kernels, copied(): pl.pallas_call(body, out_shape=jax.ShapeDtypeStruct(x.shape, x.dtype), in...  19.5 us
    unnamed x74, local copies, waits for them, and re-layouts  16.7 us
  transfers between devices with their start and end apart: 22, of which 6 were waited for; matrix products, arithmetic and copies ran while one was open for 5% of the time, Pallas kernels for 6%

profile of v3, /device:TPU:0, one launch (start us, length us, event | category | flops | bytes accessed | tf_op | source)
XLA Modules:
  0.0 643.2 jit_solution(9771953197185538575)
XLA Ops:
  0.6 471.6 %reduce_and_step.1 = (bf16[2,560,1280]{2,1,0:T(8,128)(2,1)}, bf16[2,160,4480]{2,1,0:T(8,128)(2,1)}, bf16[2,160,4480]{2,1,0:T(8,128)(2,1)}, bf16[560,1280]{1,0:T(...) custom-call(bf16[2,4480,1280]{2,1,0:T(8,128)(2,1)} %bitcast.5, ...), custom_call_target="tpu_custom_call" | custom-call | flops 1000000000 | bytes 400000000 | tf_op jit(solution)/shard_map/reduce_and_step/pallas_call | solution.py:390
  473.4 1.0 collective-permute-start.5
  475.4 1.0 collective-permute-start.20
  477.2 6.0 collective-permute-done.2.refs_2_
  485.0 1.1 collective-permute-start.8
  487.0 35.0 %collective-permute-done.3.refs_0_ = bf16[128,1280]{1,0:T(8,128)(2,1)S(1)} collective-permute-done((bf16[128,1280]{1,0:T(8,128)(2,1)S(1)}, bf16[128,1280]{1,0:T(8,128)(2,1)S(1)}, u32[]{:S(2)}, u32[]{:S(2)}) %collective-permute-start.3) | collective-permute-done | bytes 327712 | tf_op jit(solution)/shard_map/ppermute | solution.py:512
  523.0 21.1 %collective-permute-done.6.refs_1_ = bf16[128,1280]{1,0:T(8,128)(2,1)S(1)} collective-permute-done((bf16[128,1280]{1,0:T(8,128)(2,1)S(1)}, bf16[128,1280]{1,0:T(8,128)(2,1)S(1)}, u32[]{:S(2)}, u32[]{:S(2)}) %collective-permute-start.6) | collective-permute-done | bytes 327712 | tf_op jit(solution)/shard_map/ppermute | solution.py:512
  547.3 1.1 collective-permute-start.9
  550.8 18.3 %fusion.3 = (f32[2,160,4480]{2,1,0:T(8,128)}, f32[2,160,4480]{2,1,0:T(8,128)}, f32[2,160,4480]{2,1,0:T(8,128)}, f32[2,160,4480]{2,1,0:T(8,128)}) fusion(bf16[2,160,4480]{2,1,0:T(8,128)(2,1)} %get-tuple-element.36, f32[2,160,4480]{2,1,0:T(8,128)} %refs_10_.1, f32[2,160,4480]{2,1,0:T(8,128)} %refs_7_.1, bf16[2,160,4480]{2,1,0:T(8,128)(2,1)} %get-tuple-element.37, ...), kind=kLoop, calls=%fused_computation.9 | loop fusion | flops 22937600 | bytes 51609600 | tf_op jit(solution)/shard_map/add | solution.py:517
  569.1 5.0 collective-permute-done.9.refs_0_
  574.1 1.9 collective-permute-done.12.refs_1_
  576.6 1.1 copy-done.7
  578.2 11.3 %fusion.5 = (f32[2,560,1280]{2,1,0:T(8,128)}, f32[2,560,1280]{2,1,0:T(8,128)}) fusion(bf16[2,560,1280]{2,1,0:T(8,128)(2,1)} %get-tuple-element.38, f32[2,560,1280]{2,1,0:T(8,128)} %refs_9_.1, f32[2,560,1280]{2,1,0:T(8,128)} %refs_6_.1), kind=kLoop, calls=%fused_computation.11 | loop fusion | flops 11468800 | bytes 25804800 | tf_op jit(solution)/shard_map/add | solution.py:517
  589.5 1.4 copy-done.4
  590.9 3.9 placed.9.refs_6_
  594.8 8.3 %copy-done = bf16[2,1280,4480]{2,1,0:T(8,128)(2,1)S(1)} copy-done((bf16[2,1280,4480]{2,1,0:T(8,128)(2,1)S(1)}, bf16[2,1280,4480]{2,1,0:T(8,128)(2,1)}, u32[]{:S(2)}) %copy-start) | copy-done | bytes 22937624
  603.2 10.5 %copied.2 = bf16[2,1280,4480]{2,1,0:T(8,128)(2,1)} custom-call(bf16[2,1280,4480]{2,1,0:T(8,128)(2,1)S(1)} %copy-done), custom_call_target="tpu_custom_call" | custom-call | flops 100000000 | bytes 45875200 | tf_op jit(solution)/shard_map/copied/pallas_call | solution.py:463
  613.8 9.1 %copied.3.refs_4_ = bf16[2,1280,4480]{2,1,0:T(8,128)(2,1)} custom-call(bf16[2,1280,4480]{2,1,0:T(8,128)(2,1)S(1)} %bitcast.4), custom_call_target="tpu_custom_call" | custom-call | flops 100000000 | bytes 45875200 | tf_op jit(solution)/shard_map/copied/pallas_call | solution.py:463
  622.9 1.1 placed.8
  625.5 4.1 placed.10.refs_6_
  629.6 4.7 placed.11.refs_2_
  634.3 3.0 placed.12.refs_2_
  637.3 3.0 placed.13.refs_2_
  641.3 1.9 placed.15
  (108 shorter events, 15.6 us)
Async XLA Ops:
  472.3 4.2 collective-permute-start
  472.4 10.8 %collective-permute-start.2 = (bf16[128,1280]{1,0:T(8,128)(2,1)}, bf16[128,1280]{1,0:T(8,128)(2,1)S(1)}, u32[]{:S(2)}, u32[]{:S(2)}) collective-permute-start(bf16[128,1280]{1,0:T(8,128)(2,1)} %get-tuple-element.28), channel_id=1, source_target_pairs={{0,4},{1,5},{2,6},{3,7},{4,0},{5,1},{6,2},{7,3}} | collective-permute-start | bytes 983048 | tf_op jit(solution)/shard_map/ppermute | solution.py:512
  473.4 12.6 %collective-permute-start.5 = (bf16[128,1280]{1,0:T(8,128)(2,1)}, bf16[128,1280]{1,0:T(8,128)(2,1)S(1)}, u32[]{:S(2)}, u32[]{:S(2)}) collective-permute-start(bf16[128,1280]{1,0:T(8,128)(2,1)} %get-tuple-element.29), channel_id=1, source_target_pairs={{0,2},{1,3},{2,0},{3,1},{4,6},{5,7},{6,4},{7,5}} | collective-permute-start | bytes 983048 | tf_op jit(solution)/shard_map/ppermute | solution.py:512
  474.5 75.7 %collective-permute-start.18 = (bf16[560,1280]{1,0:T(8,128)(2,1)}, bf16[560,1280]{1,0:T(8,128)(2,1)S(1)}, u32[]{:S(2)}, u32[]{:S(2)}) collective-permute-start(bf16[560,1280]{1,0:T(8,128)(2,1)} %get-tuple-element.32.refs_1_), channel_id=1, source_target_pairs={{0,4},{1,5},{2,6},{3,7},{4,0},{5,1},{6,2},{7,3}} | collective-permute-start | bytes 4300808 | tf_op jit(solution)/shard_map/ppermute | solution.py:512
  475.4 74.9 %collective-permute-start.20 = (bf16[560,1280]{1,0:T(8,128)(2,1)}, bf16[560,1280]{1,0:T(8,128)(2,1)}, u32[]{:S(2)}, u32[]{:S(2)}) collective-permute-start(bf16[560,1280]{1,0:T(8,128)(2,1)} %get-tuple-element.33.refs_0_), channel_id=1, source_target_pairs={{0,2},{1,3},{2,0},{3,1},{4,6},{5,7},{6,4},{7,5}} | collective-permute-start | bytes 4300808 | tf_op jit(solution)/shard_map/ppermute | solution.py:512
  477.2 7.0 %collective-permute-start.1 = (bf16[32,4480]{1,0:T(8,128)(2,1)}, bf16[32,4480]{1,0:T(8,128)(2,1)S(1)}, u32[]{:S(2)}, u32[]{:S(2)}) collective-permute-start(bf16[32,4480]{1,0:T(8,128)(2,1)} %get-tuple-element.26.refs_1_), channel_id=1, source_target_pairs={{0,1},{1,0},{2,3},{3,2},{4,5},{5,4},{6,7},{7,6}} | collective-permute-start | bytes 860168 | tf_op jit(solution)/shard_map/ppermute | solution.py:512
  483.2 38.7 %collective-permute-start.3 = (bf16[128,1280]{1,0:T(8,128)(2,1)S(1)}, bf16[128,1280]{1,0:T(8,128)(2,1)S(1)}, u32[]{:S(2)}, u32[]{:S(2)}) collective-permute-start(bf16[128,1280]{1,0:T(8,128)(2,1)S(1)} %collective-permute-done.2.refs_2_), channel_id=1, source_target_pairs={{0,2},{1,3},{2,0},{3,1},{4,6},{5,7},{6,4},{7,5}} | collective-permute-start | bytes 983048 | tf_op jit(solution)/shard_map/ppermute | solution.py:512
  485.0 62.4 %collective-permute-start.8 = (bf16[432,1280]{1,0:T(8,128)(2,1)}, bf16[432,1280]{1,0:T(8,128)(2,1)S(1)}, u32[]{:S(2)}, u32[]{:S(2)}) collective-permute-start(bf16[432,1280]{1,0:T(8,128)(2,1)} %get-tuple-element.30), channel_id=1, source_target_pairs={{0,4},{1,5},{2,6},{3,7},{4,0},{5,1},{6,2},{7,3}} | collective-permute-start | bytes 3317768 | tf_op jit(solution)/shard_map/ppermute | solution.py:512
  486.0 63.2 %collective-permute-start.11 = (bf16[432,1280]{1,0:T(8,128)(2,1)}, bf16[432,1280]{1,0:T(8,128)(2,1)S(1)}, u32[]{:S(2)}, u32[]{:S(2)}) collective-permute-start(bf16[432,1280]{1,0:T(8,128)(2,1)} %get-tuple-element.31), channel_id=1, source_target_pairs={{0,2},{1,3},{2,0},{3,1},{4,6},{5,7},{6,4},{7,5}} | collective-permute-start | bytes 3317768 | tf_op jit(solution)/shard_map/ppermute | solution.py:512
  522.0 28.4 %copy-start.13 = (bf16[128,1280]{1,0:T(8,128)(2,1)}, bf16[128,1280]{1,0:T(8,128)(2,1)S(1)}, u32[]{:S(2)}) copy-start(bf16[128,1280]{1,0:T(8,128)(2,1)S(1)} %collective-permute-done.3.refs_0_) | copy-start | bytes 983044
  522.0 22.1 %collective-permute-start.6 = (bf16[128,1280]{1,0:T(8,128)(2,1)S(1)}, bf16[128,1280]{1,0:T(8,128)(2,1)S(1)}, u32[]{:S(2)}, u32[]{:S(2)}) collective-permute-start(bf16[128,1280]{1,0:T(8,128)(2,1)S(1)} %collective-permute-done.5.refs_3_), channel_id=1, source_target_pairs={{0,4},{1,5},{2,6},{3,7},{4,0},{5,1},{6,2},{7,3}} | collective-permute-start | bytes 983048 | tf_op jit(solution)/shard_map/ppermute | solution.py:512
  544.1 1.6 collective-permute-start.16
  546.5 1.9 collective-permute-start.17
  547.3 26.8 %collective-permute-start.9 = (bf16[432,1280]{1,0:T(8,128)(2,1)S(1)}, bf16[432,1280]{1,0:T(8,128)(2,1)}, u32[]{:S(2)}, u32[]{:S(2)}) collective-permute-start(bf16[432,1280]{1,0:T(8,128)(2,1)S(1)} %collective-permute-done.8.refs_0_), channel_id=1, source_target_pairs={{0,2},{1,3},{2,0},{3,1},{4,6},{5,7},{6,4},{7,5}} | collective-permute-start | bytes 3317768 | tf_op jit(solution)/shard_map/ppermute | solution.py:512
  549.1 26.9 %collective-permute-start.14 = (bf16[432,1280]{1,0:T(8,128)(2,1)S(1)}, bf16[432,1280]{1,0:T(8,128)(2,1)}, u32[]{:S(2)}, u32[]{:S(2)}) collective-permute-start(bf16[432,1280]{1,0:T(8,128)(2,1)S(1)} %collective-permute-done.8.refs_0_), channel_id=1, source_target_pairs={{0,1},{1,0},{2,3},{3,2},{4,5},{5,4},{6,7},{7,6}} | collective-permute-start | bytes 3317768 | tf_op jit(solution)/shard_map/ppermute | solution.py:512
  549.2 26.8 %collective-permute-start.12 = (bf16[432,1280]{1,0:T(8,128)(2,1)S(1)}, bf16[432,1280]{1,0:T(8,128)(2,1)}, u32[]{:S(2)}, u32[]{:S(2)}) collective-permute-start(bf16[432,1280]{1,0:T(8,128)(2,1)S(1)} %collective-permute-done.11.refs_1_), channel_id=1, source_target_pairs={{0,4},{1,5},{2,6},{3,7},{4,0},{5,1},{6,2},{7,3}} | collective-permute-start | bytes 3317768 | tf_op jit(solution)/shard_map/ppermute | solution.py:512
  550.2 26.4 %collective-permute-start.15 = (bf16[432,1280]{1,0:T(8,128)(2,1)S(1)}, bf16[432,1280]{1,0:T(8,128)(2,1)}, u32[]{:S(2)}, u32[]{:S(2)}) collective-permute-start(bf16[432,1280]{1,0:T(8,128)(2,1)S(1)} %collective-permute-done.11.refs_1_), channel_id=1, source_target_pairs={{0,1},{1,0},{2,3},{3,2},{4,5},{5,4},{6,7},{7,6}} | collective-permute-start | bytes 3317768 | tf_op jit(solution)/shard_map/ppermute | solution.py:512
  550.4 26.2 %collective-permute-start.19 = (bf16[560,1280]{1,0:T(8,128)(2,1)S(1)}, bf16[560,1280]{1,0:T(8,128)(2,1)S(1)}, u32[]{:S(2)}, u32[]{:S(2)}) collective-permute-start(bf16[560,1280]{1,0:T(8,128)(2,1)S(1)} %collective-permute-done.18.refs_4_), channel_id=1, source_target_pairs={{0,1},{1,0},{2,3},{3,2},{4,5},{5,4},{6,7},{7,6}} | collective-permute-start | bytes 4300808 | tf_op jit(solution)/shard_map/ppermute | solution.py:512
  574.1 67.1 %collective-permute-start.4 = (bf16[128,1280]{1,0:T(8,128)(2,1)}, bf16[128,1280]{1,0:T(8,128)(2,1)}, u32[]{:S(2)}, u32[]{:S(2)}) collective-permute-start(bf16[128,1280]{1,0:T(8,128)(2,1)} %copy-done.13), channel_id=1, source_target_pairs={{0,1},{1,0},{2,3},{3,2},{4,5},{5,4},{6,7},{7,6}} | collective-permute-start | bytes 983048 | tf_op jit(solution)/shard_map/ppermute | solution.py:512
  576.0 65.2 %collective-permute-start.7 = (bf16[128,1280]{1,0:T(8,128)(2,1)}, bf16[128,1280]{1,0:T(8,128)(2,1)}, u32[]{:S(2)}, u32[]{:S(2)}) collective-permute-start(bf16[128,1280]{1,0:T(8,128)(2,1)} %copy-done.19), channel_id=1, source_target_pairs={{0,1},{1,0},{2,3},{3,2},{4,5},{5,4},{6,7},{7,6}} | collective-permute-start | bytes 983048 | tf_op jit(solution)/shard_map/ppermute | solution.py:512
  576.0 53.5 %collective-permute-start.21 = (bf16[560,1280]{1,0:T(8,128)(2,1)}, bf16[560,1280]{1,0:T(8,128)(2,1)}, u32[]{:S(2)}, u32[]{:S(2)}) collective-permute-start(bf16[560,1280]{1,0:T(8,128)(2,1)} %collective-permute-done.20.refs_5_), channel_id=1, source_target_pairs={{0,1},{1,0},{2,3},{3,2},{4,5},{5,4},{6,7},{7,6}} | collective-permute-start | bytes 4300808 | tf_op jit(solution)/shard_map/ppermute | solution.py:512
  576.6 60.7 %collective-permute-start.10 = (bf16[432,1280]{1,0:T(8,128)(2,1)}, bf16[432,1280]{1,0:T(8,128)(2,1)}, u32[]{:S(2)}, u32[]{:S(2)}) collective-permute-start(bf16[432,1280]{1,0:T(8,128)(2,1)} %collective-permute-done.9.refs_0_), channel_id=1, source_target_pairs={{0,1},{1,0},{2,3},{3,2},{4,5},{5,4},{6,7},{7,6}} | collective-permute-start | bytes 3317768 | tf_op jit(solution)/shard_map/ppermute | solution.py:512
  577.7 59.6 %collective-permute-start.13 = (bf16[432,1280]{1,0:T(8,128)(2,1)}, bf16[432,1280]{1,0:T(8,128)(2,1)}, u32[]{:S(2)}, u32[]{:S(2)}) collective-permute-start(bf16[432,1280]{1,0:T(8,128)(2,1)} %collective-permute-done.12.refs_1_), channel_id=1, source_target_pairs={{0,1},{1,0},{2,3},{3,2},{4,5},{5,4},{6,7},{7,6}} | collective-permute-start | bytes 3317768 | tf_op jit(solution)/shard_map/ppermute | solution.py:512
  590.9 22.8 %slice-start.2 = ((s8[22937600]{0:T(1024)(128)(4,1)}), s8[4194304]{0:T(1024)(128)(4,1)S(1)}, s32[]{:S(2)}) async-start(s8[22937600]{0:T(1024)(128)(4,1)} %bitcast.3), calls=%async_computation.2 | async-start | bytes 8388608
  (35 other events, 259.3 us)

commit v4 on v3

--- a/solution.py
+++ b/solution.py
@@ -13,7 +13,7 @@
 X, Y, CORE = 4, 2, 1
 LANES = 640
 ROWS = 16
-RING = 6
+RING = 5
 
 
 class Weight:
@@ -174,7 +174,7 @@
         wt = plan[t][0]
         dst = new[wt].at[layer, rows(t, me)] if weights[wt].gathered else new[wt][6 + layer].at[mine(t)]
         k = number(layer)
-        return pltpu.make_async_remote_copy(held(t, new3, layer), dst, own_send.at[t % 2, k, i], own_recv.at[t % RING, k, i], **to(masks[i]))
+        return pltpu.make_async_remote_copy(held(t, new3, layer), dst, own_send.at[t % 2, k, i], own_recv.at[t % (RING + 1), k, i], **to(masks[i]))
 
     def own_copies(t):
         if not gathered(t):
@@ -191,12 +191,11 @@
         source, target = ((X, Y), (Y, X))[layer]
         return pass_copy(t, layer, source, target, hop_send.at[t % RING, layer], hop_recv.at[t % RING, layer], late[layer] if t == steps - 1 else None)
 
-    def twin(t, layer, i):
-        k = number(layer)
-        return pass_copy(t, layer, masks[i], CORE, twin_send.at[t % RING, k, i], twin_recv.at[t % RING, k, i])
-
-    def twin2(t, layer):
-        return pass_copy(t, layer, X ^ Y, CORE, twin2_send.at[t % RING, layer], twin2_recv.at[t % RING, layer])
+    def twin(t, i):
+        return pass_copy(t, pl.ds(0, 2), masks[i], CORE, twin_send.at[t % RING, i], twin_recv.at[t % RING, i])
+
+    def twin2(t):
+        return pass_copy(t, pl.ds(0, 2), X ^ Y, CORE, twin2_send.at[t % RING], twin2_recv.at[t % RING])
 
     def real(t):
         return 0 <= t < steps
@@ -322,22 +321,20 @@
                     own_copy(c3, layers(c3)[0], i).wait_recv()
                 for layer in range(2):
                     hop(c3, layer).start()
-                for i in range(2):
-                    twin(c3, layers(c3)[0], i).start()
             else:
                 for layer in range(2):
                     own_copy(c3, layer, layer).wait_recv()
                     hop(c3, layer).start()
-                    twin(c3, layer, layer).start()
                 for layer in range(2):
                     own_copy(c3, layer, 1 - layer).wait_recv()
-                    twin(c3, layer, 1 - layer).start()
+            for i in range(2):
+                twin(c3, i).start()
         c4 = t - 4
         if gathered(c4):
             for layer in range(2):
                 hop(c4, layer).wait_recv()
-                if c4 < steps - 1:
-                    twin2(c4, layer).start()
+            if c4 < steps - 1:
+                twin2(c4).start()
 
         if real(c4):
             for layer in layers(c4):
@@ -345,13 +342,12 @@
         c5 = t - 5
         if real(c5):
             if gathered(c5):
-                for layer in layers(c5):
-                    for i in range(2):
-                        twin(c5, layer, i).wait()
+                for i in range(2):
+                    twin(c5, i).wait()
                 for layer in range(2):
                     hop(c5, layer).wait_send()
-                    if c5 < steps - 1:
-                        twin2(c5, layer).wait()
+                if c5 < steps - 1:
+                    twin2(c5).wait()
 
     for u in range(4):
         soon(u).wait_send()
@@ -415,13 +411,13 @@
             dma((2, 7)),
             dma((2, 2, 3)),
             dma((2, 2, 3)),
-            dma((RING, 2, 3)),
+            dma((RING + 1, 2, 3)),
             dma((RING, 2)),
             dma((RING, 2)),
-            dma((RING, 2, 2)),
-            dma((RING, 2, 2)),
             dma((RING, 2)),
             dma((RING, 2)),
+            dma((RING,)),
+            dma((RING,)),
         ],
         compiler_params=pltpu.CompilerParams(collective_id=0, has_side_effects=True, vmem_limit_bytes=60 << 20),
         cost_estimate=pl.CostEstimate(flops=10**9, bytes_accessed=4 * 10**8, transcendentals=10**7),

time: 644 us -> 644 us (level)
  no operation moved by 1% of the time
where the time goes in v4:
time: 644 us; the launch traced here: 643 us
  Pallas kernels  513 us (80%)
  waiting for transfers between devices  70 us (11%)
  other arithmetic  29.6 us (5%)
  local copies, waits for them, and re-layouts  16.7 us (3%)
  starting transfers between devices  12.1 us (2%)
    pallas_call x1, Pallas kernels, reduce_and_step(): pl.pallas_call(functools.partial(step_kernel, weights), out_shape=out_sha...  471 us
    ppermute x22, waiting for transfers between devices, moved(): return lax.ppermute(x, 'dp', [(i, i ^ mask) for i in range(8)])  70 us
    add x2, other arithmetic, moments(): return (0.9 * m + 0.1 * g, 0.95 * v + 0.05 * g * g)  29.6 us
    pallas_call x8, Pallas kernels, placed(): pl.pallas_call(body, out_shape=jax.ShapeDtypeStruct((2, block * 8, cols),...  22.6 us
    pallas_call x2, Pallas kernels, copied(): pl.pallas_call(body, out_shape=jax.ShapeDtypeStruct(x.shape, x.dtype), in...  19.5 us
    unnamed x74, local copies, waits for them, and re-layouts  16.7 us
  transfers between devices with their start and end apart: 22, of which 6 were waited for; matrix products, arithmetic and copies ran while one was open for 5% of the time, Pallas kernels for 6%

profile of v4, /device:TPU:0, one launch (start us, length us, event | category | flops | bytes accessed | tf_op | source)
XLA Modules:
  0.0 642.7 jit_solution(3006301994428574434)
XLA Ops:
  0.6 471.1 %reduce_and_step.1 = (bf16[2,560,1280]{2,1,0:T(8,128)(2,1)}, bf16[2,160,4480]{2,1,0:T(8,128)(2,1)}, bf16[2,160,4480]{2,1,0:T(8,128)(2,1)}, bf16[560,1280]{1,0:T(...) custom-call(bf16[2,4480,1280]{2,1,0:T(8,128)(2,1)} %bitcast.5, ...), custom_call_target="tpu_custom_call" | custom-call | flops 1000000000 | bytes 400000000 | tf_op jit(solution)/shard_map/reduce_and_step/pallas_call | solution.py:386
  472.9 1.0 collective-permute-start.5
  474.9 1.0 collective-permute-start.20
  476.7 6.0 collective-permute-done.2.refs_2_
  484.4 1.1 collective-permute-start.8
  486.4 35.0 %collective-permute-done.3.refs_0_ = bf16[128,1280]{1,0:T(8,128)(2,1)S(1)} collective-permute-done((bf16[128,1280]{1,0:T(8,128)(2,1)S(1)}, bf16[128,1280]{1,0:T(8,128)(2,1)S(1)}, u32[]{:S(2)}, u32[]{:S(2)}) %collective-permute-start.3) | collective-permute-done | bytes 327712 | tf_op jit(solution)/shard_map/ppermute | solution.py:508
  522.4 21.1 %collective-permute-done.6.refs_1_ = bf16[128,1280]{1,0:T(8,128)(2,1)S(1)} collective-permute-done((bf16[128,1280]{1,0:T(8,128)(2,1)S(1)}, bf16[128,1280]{1,0:T(8,128)(2,1)S(1)}, u32[]{:S(2)}, u32[]{:S(2)}) %collective-permute-start.6) | collective-permute-done | bytes 327712 | tf_op jit(solution)/shard_map/ppermute | solution.py:508
  546.8 1.1 collective-permute-start.9
  550.2 18.3 %fusion.3 = (f32[2,160,4480]{2,1,0:T(8,128)}, f32[2,160,4480]{2,1,0:T(8,128)}, f32[2,160,4480]{2,1,0:T(8,128)}, f32[2,160,4480]{2,1,0:T(8,128)}) fusion(bf16[2,160,4480]{2,1,0:T(8,128)(2,1)} %get-tuple-element.36, f32[2,160,4480]{2,1,0:T(8,128)} %refs_10_.1, f32[2,160,4480]{2,1,0:T(8,128)} %refs_7_.1, bf16[2,160,4480]{2,1,0:T(8,128)(2,1)} %get-tuple-element.37, ...), kind=kLoop, calls=%fused_computation.9 | loop fusion | flops 22937600 | bytes 51609600 | tf_op jit(solution)/shard_map/add | solution.py:513
  568.5 5.0 collective-permute-done.9.refs_0_
  573.6 1.9 collective-permute-done.12.refs_1_
  576.0 1.1 copy-done.7
  577.7 11.3 %fusion.5 = (f32[2,560,1280]{2,1,0:T(8,128)}, f32[2,560,1280]{2,1,0:T(8,128)}) fusion(bf16[2,560,1280]{2,1,0:T(8,128)(2,1)} %get-tuple-element.38, f32[2,560,1280]{2,1,0:T(8,128)} %refs_9_.1, f32[2,560,1280]{2,1,0:T(8,128)} %refs_6_.1), kind=kLoop, calls=%fused_computation.11 | loop fusion | flops 11468800 | bytes 25804800 | tf_op jit(solution)/shard_map/add | solution.py:513
  589.0 1.4 copy-done.4
  590.3 3.9 placed.9.refs_6_
  594.3 8.3 %copy-done = bf16[2,1280,4480]{2,1,0:T(8,128)(2,1)S(1)} copy-done((bf16[2,1280,4480]{2,1,0:T(8,128)(2,1)S(1)}, bf16[2,1280,4480]{2,1,0:T(8,128)(2,1)}, u32[]{:S(2)}) %copy-start) | copy-done | bytes 22937624
  602.6 10.5 %copied.2 = bf16[2,1280,4480]{2,1,0:T(8,128)(2,1)} custom-call(bf16[2,1280,4480]{2,1,0:T(8,128)(2,1)S(1)} %copy-done), custom_call_target="tpu_custom_call" | custom-call | flops 100000000 | bytes 45875200 | tf_op jit(solution)/shard_map/copied/pallas_call | solution.py:459
  613.2 9.1 %copied.3.refs_4_ = bf16[2,1280,4480]{2,1,0:T(8,128)(2,1)} custom-call(bf16[2,1280,4480]{2,1,0:T(8,128)(2,1)S(1)} %bitcast.4), custom_call_target="tpu_custom_call" | custom-call | flops 100000000 | bytes 45875200 | tf_op jit(solution)/shard_map/copied/pallas_call | solution.py:459
  622.4 1.1 placed.8
  624.9 4.1 placed.10.refs_6_
  629.1 4.7 placed.11.refs_2_
  633.7 3.0 placed.12.refs_2_
  636.7 3.0 placed.13.refs_2_
  640.7 1.9 placed.15
  (108 shorter events, 15.6 us)
Async XLA Ops:
  471.7 4.2 collective-permute-start
  471.9 10.8 %collective-permute-start.2 = (bf16[128,1280]{1,0:T(8,128)(2,1)}, bf16[128,1280]{1,0:T(8,128)(2,1)S(1)}, u32[]{:S(2)}, u32[]{:S(2)}) collective-permute-start(bf16[128,1280]{1,0:T(8,128)(2,1)} %get-tuple-element.28), channel_id=1, source_target_pairs={{0,4},{1,5},{2,6},{3,7},{4,0},{5,1},{6,2},{7,3}} | collective-permute-start | bytes 983048 | tf_op jit(solution)/shard_map/ppermute | solution.py:508
  472.9 12.6 %collective-permute-start.5 = (bf16[128,1280]{1,0:T(8,128)(2,1)}, bf16[128,1280]{1,0:T(8,128)(2,1)S(1)}, u32[]{:S(2)}, u32[]{:S(2)}) collective-permute-start(bf16[128,1280]{1,0:T(8,128)(2,1)} %get-tuple-element.29), channel_id=1, source_target_pairs={{0,2},{1,3},{2,0},{3,1},{4,6},{5,7},{6,4},{7,5}} | collective-permute-start | bytes 983048 | tf_op jit(solution)/shard_map/ppermute | solution.py:508
  473.9 75.7 %collective-permute-start.18 = (bf16[560,1280]{1,0:T(8,128)(2,1)}, bf16[560,1280]{1,0:T(8,128)(2,1)S(1)}, u32[]{:S(2)}, u32[]{:S(2)}) collective-permute-start(bf16[560,1280]{1,0:T(8,128)(2,1)} %get-tuple-element.32.refs_1_), channel_id=1, source_target_pairs={{0,4},{1,5},{2,6},{3,7},{4,0},{5,1},{6,2},{7,3}} | collective-permute-start | bytes 4300808 | tf_op jit(solution)/shard_map/ppermute | solution.py:508
  474.9 74.9 %collective-permute-start.20 = (bf16[560,1280]{1,0:T(8,128)(2,1)}, bf16[560,1280]{1,0:T(8,128)(2,1)}, u32[]{:S(2)}, u32[]{:S(2)}) collective-permute-start(bf16[560,1280]{1,0:T(8,128)(2,1)} %get-tuple-element.33.refs_0_), channel_id=1, source_target_pairs={{0,2},{1,3},{2,0},{3,1},{4,6},{5,7},{6,4},{7,5}} | collective-permute-start | bytes 4300808 | tf_op jit(solution)/shard_map/ppermute | solution.py:508
  476.7 7.0 %collective-permute-start.1 = (bf16[32,4480]{1,0:T(8,128)(2,1)}, bf16[32,4480]{1,0:T(8,128)(2,1)S(1)}, u32[]{:S(2)}, u32[]{:S(2)}) collective-permute-start(bf16[32,4480]{1,0:T(8,128)(2,1)} %get-tuple-element.26.refs_1_), channel_id=1, source_target_pairs={{0,1},{1,0},{2,3},{3,2},{4,5},{5,4},{6,7},{7,6}} | collective-permute-start | bytes 860168 | tf_op jit(solution)/shard_map/ppermute | solution.py:508
  482.7 38.7 %collective-permute-start.3 = (bf16[128,1280]{1,0:T(8,128)(2,1)S(1)}, bf16[128,1280]{1,0:T(8,128)(2,1)S(1)}, u32[]{:S(2)}, u32[]{:S(2)}) collective-permute-start(bf16[128,1280]{1,0:T(8,128)(2,1)S(1)} %collective-permute-done.2.refs_2_), channel_id=1, source_target_pairs={{0,2},{1,3},{2,0},{3,1},{4,6},{5,7},{6,4},{7,5}} | collective-permute-start | bytes 983048 | tf_op jit(solution)/shard_map/ppermute | solution.py:508
  484.4 62.4 %collective-permute-start.8 = (bf16[432,1280]{1,0:T(8,128)(2,1)}, bf16[432,1280]{1,0:T(8,128)(2,1)S(1)}, u32[]{:S(2)}, u32[]{:S(2)}) collective-permute-start(bf16[432,1280]{1,0:T(8,128)(2,1)} %get-tuple-element.30), channel_id=1, source_target_pairs={{0,4},{1,5},{2,6},{3,7},{4,0},{5,1},{6,2},{7,3}} | collective-permute-start | bytes 3317768 | tf_op jit(solution)/shard_map/ppermute | solution.py:508
  485.5 63.2 %collective-permute-start.11 = (bf16[432,1280]{1,0:T(8,128)(2,1)}, bf16[432,1280]{1,0:T(8,128)(2,1)S(1)}, u32[]{:S(2)}, u32[]{:S(2)}) collective-permute-start(bf16[432,1280]{1,0:T(8,128)(2,1)} %get-tuple-element.31), channel_id=1, source_target_pairs={{0,2},{1,3},{2,0},{3,1},{4,6},{5,7},{6,4},{7,5}} | collective-permute-start | bytes 3317768 | tf_op jit(solution)/shard_map/ppermute | solution.py:508
  521.4 28.4 %copy-start.13 = (bf16[128,1280]{1,0:T(8,128)(2,1)}, bf16[128,1280]{1,0:T(8,128)(2,1)S(1)}, u32[]{:S(2)}) copy-start(bf16[128,1280]{1,0:T(8,128)(2,1)S(1)} %collective-permute-done.3.refs_0_) | copy-start | bytes 983044
  521.4 22.1 %collective-permute-start.6 = (bf16[128,1280]{1,0:T(8,128)(2,1)S(1)}, bf16[128,1280]{1,0:T(8,128)(2,1)S(1)}, u32[]{:S(2)}, u32[]{:S(2)}) collective-permute-start(bf16[128,1280]{1,0:T(8,128)(2,1)S(1)} %collective-permute-done.5.refs_3_), channel_id=1, source_target_pairs={{0,4},{1,5},{2,6},{3,7},{4,0},{5,1},{6,2},{7,3}} | collective-permute-start | bytes 983048 | tf_op jit(solution)/shard_map/ppermute | solution.py:508
  543.5 1.6 collective-permute-start.16
  545.9 1.9 collective-permute-start.17
  546.8 26.8 %collective-permute-start.9 = (bf16[432,1280]{1,0:T(8,128)(2,1)S(1)}, bf16[432,1280]{1,0:T(8,128)(2,1)}, u32[]{:S(2)}, u32[]{:S(2)}) collective-permute-start(bf16[432,1280]{1,0:T(8,128)(2,1)S(1)} %collective-permute-done.8.refs_0_), channel_id=1, source_target_pairs={{0,2},{1,3},{2,0},{3,1},{4,6},{5,7},{6,4},{7,5}} | collective-permute-start | bytes 3317768 | tf_op jit(solution)/shard_map/ppermute | solution.py:508
  548.6 26.9 %collective-permute-start.14 = (bf16[432,1280]{1,0:T(8,128)(2,1)S(1)}, bf16[432,1280]{1,0:T(8,128)(2,1)}, u32[]{:S(2)}, u32[]{:S(2)}) collective-permute-start(bf16[432,1280]{1,0:T(8,128)(2,1)S(1)} %collective-permute-done.8.refs_0_), channel_id=1, source_target_pairs={{0,1},{1,0},{2,3},{3,2},{4,5},{5,4},{6,7},{7,6}} | collective-permute-start | bytes 3317768 | tf_op jit(solution)/shard_map/ppermute | solution.py:508
  548.7 26.8 %collective-permute-start.12 = (bf16[432,1280]{1,0:T(8,128)(2,1)S(1)}, bf16[432,1280]{1,0:T(8,128)(2,1)}, u32[]{:S(2)}, u32[]{:S(2)}) collective-permute-start(bf16[432,1280]{1,0:T(8,128)(2,1)S(1)} %collective-permute-done.11.refs_1_), channel_id=1, source_target_pairs={{0,4},{1,5},{2,6},{3,7},{4,0},{5,1},{6,2},{7,3}} | collective-permute-start | bytes 3317768 | tf_op jit(solution)/shard_map/ppermute | solution.py:508
  549.6 26.4 %collective-permute-start.15 = (bf16[432,1280]{1,0:T(8,128)(2,1)S(1)}, bf16[432,1280]{1,0:T(8,128)(2,1)}, u32[]{:S(2)}, u32[]{:S(2)}) collective-permute-start(bf16[432,1280]{1,0:T(8,128)(2,1)S(1)} %collective-permute-done.11.refs_1_), channel_id=1, source_target_pairs={{0,1},{1,0},{2,3},{3,2},{4,5},{5,4},{6,7},{7,6}} | collective-permute-start | bytes 3317768 | tf_op jit(solution)/shard_map/ppermute | solution.py:508
  549.8 26.2 %collective-permute-start.19 = (bf16[560,1280]{1,0:T(8,128)(2,1)S(1)}, bf16[560,1280]{1,0:T(8,128)(2,1)S(1)}, u32[]{:S(2)}, u32[]{:S(2)}) collective-permute-start(bf16[560,1280]{1,0:T(8,128)(2,1)S(1)} %collective-permute-done.18.refs_4_), channel_id=1, source_target_pairs={{0,1},{1,0},{2,3},{3,2},{4,5},{5,4},{6,7},{7,6}} | collective-permute-start | bytes 4300808 | tf_op jit(solution)/shard_map/ppermute | solution.py:508
  573.6 67.1 %collective-permute-start.4 = (bf16[128,1280]{1,0:T(8,128)(2,1)}, bf16[128,1280]{1,0:T(8,128)(2,1)}, u32[]{:S(2)}, u32[]{:S(2)}) collective-permute-start(bf16[128,1280]{1,0:T(8,128)(2,1)} %copy-done.13), channel_id=1, source_target_pairs={{0,1},{1,0},{2,3},{3,2},{4,5},{5,4},{6,7},{7,6}} | collective-permute-start | bytes 983048 | tf_op jit(solution)/shard_map/ppermute | solution.py:508
  575.5 65.2 %collective-permute-start.7 = (bf16[128,1280]{1,0:T(8,128)(2,1)}, bf16[128,1280]{1,0:T(8,128)(2,1)}, u32[]{:S(2)}, u32[]{:S(2)}) collective-permute-start(bf16[128,1280]{1,0:T(8,128)(2,1)} %copy-done.19), channel_id=1, source_target_pairs={{0,1},{1,0},{2,3},{3,2},{4,5},{5,4},{6,7},{7,6}} | collective-permute-start | bytes 983048 | tf_op jit(solution)/shard_map/ppermute | solution.py:508
  575.5 53.5 %collective-permute-start.21 = (bf16[560,1280]{1,0:T(8,128)(2,1)}, bf16[560,1280]{1,0:T(8,128)(2,1)}, u32[]{:S(2)}, u32[]{:S(2)}) collective-permute-start(bf16[560,1280]{1,0:T(8,128)(2,1)} %collective-permute-done.20.refs_5_), channel_id=1, source_target_pairs={{0,1},{1,0},{2,3},{3,2},{4,5},{5,4},{6,7},{7,6}} | collective-permute-start | bytes 4300808 | tf_op jit(solution)/shard_map/ppermute | solution.py:508
  576.0 60.7 %collective-permute-start.10 = (bf16[432,1280]{1,0:T(8,128)(2,1)}, bf16[432,1280]{1,0:T(8,128)(2,1)}, u32[]{:S(2)}, u32[]{:S(2)}) collective-permute-start(bf16[432,1280]{1,0:T(8,128)(2,1)} %collective-permute-done.9.refs_0_), channel_id=1, source_target_pairs={{0,1},{1,0},{2,3},{3,2},{4,5},{5,4},{6,7},{7,6}} | collective-permute-start | bytes 3317768 | tf_op jit(solution)/shard_map/ppermute | solution.py:508
  577.2 59.6 %collective-permute-start.13 = (bf16[432,1280]{1,0:T(8,128)(2,1)}, bf16[432,1280]{1,0:T(8,128)(2,1)}, u32[]{:S(2)}, u32[]{:S(2)}) collective-permute-start(bf16[432,1280]{1,0:T(8,128)(2,1)} %collective-permute-done.12.refs_1_), channel_id=1, source_target_pairs={{0,1},{1,0},{2,3},{3,2},{4,5},{5,4},{6,7},{7,6}} | collective-permute-start | bytes 3317768 | tf_op jit(solution)/shard_map/ppermute | solution.py:508
  590.3 22.8 %slice-start.2 = ((s8[22937600]{0:T(1024)(128)(4,1)}), s8[4194304]{0:T(1024)(128)(4,1)S(1)}, s32[]{:S(2)}) async-start(s8[22937600]{0:T(1024)(128)(4,1)} %bitcast.3), calls=%async_computation.2 | async-start | bytes 8388608
  (35 other events, 259.3 us)
